TPU v7x, 32 devices: a whole 2x2x4 slice. The times are simulated.
32 devices in a mesh: dp: 8 (over z, y), tensor: 4 (over x, core).
Axes of the slice: x: 2, y: 2, z: 4, core: 2. Of those that a mesh axis runs over, the one named last changes fastest.
Arguments:
- patches: bfloat16 [8192, 1280], P('dp', 'tensor'), may hold values from -60 to 60
- counts: int32 [16], replicated, may hold values from 0 to 512, as said below
- first_gain: float32 [1280], replicated, may hold values from 0.1 to 1.9
- first_shift: float32 [1280], replicated, may hold values from -3 to 3
- in_weight: bfloat16 [1280, 3, 1280], P(None, None, 'tensor'), may hold values from -0.15625 to 0.15625
- in_bias: float32 [3, 1280], P(None, 'tensor'), may hold values from -30 to 30
- out_weight: bfloat16 [1280, 1280], P(None, 'tensor'), may hold values from -0.15625 to 0.15625
- out_bias: float32 [1280], P('tensor'), may hold values from -3 to 3
- second_gain: float32 [1280], P('tensor'), may hold values from 0.1 to 1.9
- second_shift: float32 [1280], P('tensor'), may hold values from -3 to 3
- merger_weight: bfloat16 [4, 1280, 4096], P(None, 'tensor', 'dp'), may hold values from -0.078125 to 0.078125
- merger_bias: float32 [4096], replicated, may hold values from -4 to 4
Outputs:
- embeds: bfloat16 [2048, 4096], P(('dp', 'tensor'))
Inputs may be any that keep to these rules, and one draw needn't show every extreme that they name: Entry 2 r + j is the patch count of slot j of data rank r, 0 for an empty slot; a rank's images fill its slots from slot 0; counts are multiples of 4; ranks 2 i and 2 i + 1 hold at most two images together, and in every draw some rank holds two.
All inputs are finite; a program needn't handle non-finite values.
Results may differ from a plain program's by a relative error of at most 0.0095.
Values may be sent and summed in bfloat16 or wider, within the bound.
No kernel may reach another device: no remote copies, remote signals or barrier semaphores. Data moves between devices by JAX's collectives and lax.ppermute only.
A program may use at most 128 MiB of HBM per device.

v0:
```python
import functools
import math

import jax
import jax.numpy as jnp
from jax import lax
from jax.experimental import pallas as pl
from jax.experimental.pallas import tpu as pltpu
from jax.sharding import PartitionSpec as P

D = 1280
HEADS = 16
TILE = 512
SLOTS = 2
MERGE = 4

EPS = 1e-06
MASKED = -1e30


def swap(x, dp_flip=0, tensor_flip=0):
    width = lax.axis_size("tensor")
    total = lax.axis_size("dp") * width
    flip = dp_flip * width + tensor_flip
    return lax.ppermute(x, ("dp", "tensor"), [(i, i ^ flip) for i in range(total)])


def attend_kernel(scalars, own, near, far, cross, gain, shift, weight, bias, order, out, normed):
    me = scalars[0]
    count = scalars[1]
    rows, width = own.shape
    head_size = D // HEADS
    heads = width // head_size
    step = 32
    odd = jnp.bitwise_and(me, 1) == 1
    upper = jnp.bitwise_and(me, 2) == 2
    for start in range(0, rows, step):
        part = pl.ds(start, step)
        blocks = [r[part, :].astype(jnp.float32) for r in (own, near, far, cross)]
        mean = sum(jnp.sum(b, axis=1, keepdims=True) for b in blocks) / D
        centred = [b - mean for b in blocks]
        spread = sum(jnp.sum(c * c, axis=1, keepdims=True) for c in centred) / D
        inverse = lax.rsqrt(spread + EPS)
        p, q, r, s = [c * inverse for c in centred]
        p, q, r, s = jnp.where(odd, q, p), jnp.where(odd, p, q), jnp.where(odd, s, r), jnp.where(odd, r, s)
        p, q, r, s = jnp.where(upper, r, p), jnp.where(upper, s, q), jnp.where(upper, p, r), jnp.where(upper, q, s)
        line = jnp.concatenate([p, q, r, s], axis=1)
        normed[part, :] = (line * gain[...] + shift[...]).astype(jnp.bfloat16)
    projected = lax.dot_general(
        weight[...], normed[...], (((1,), (1,)), ((), ())), preferred_element_type=jnp.float32
    )
    projected = (projected + bias[...]).astype(jnp.bfloat16)
    queries = jnp.dot(
        projected[:width], order[...], preferred_element_type=jnp.float32
    ).astype(jnp.bfloat16)
    live = lax.broadcasted_iota(jnp.int32, (rows, rows), 0) < count
    scale = math.log2(math.e) / math.sqrt(head_size)
    for h in range(heads):
        a, b = h * head_size, (h + 1) * head_size
        scores = lax.dot_general(
            projected[width + a : width + b], queries[a:b], (((0,), (0,)), ((), ())),
            preferred_element_type=jnp.float32,
        )
        scores = jnp.where(live, scores, MASKED)
        highest = jnp.max(scores, axis=0, keepdims=True)
        raised = jnp.exp2((scores - highest) * scale)
        total = jnp.sum(raised, axis=0, keepdims=True)
        mixed = jnp.dot(
            projected[2 * width + a : 2 * width + b], raised.astype(jnp.bfloat16),
            preferred_element_type=jnp.float32,
        )
        out[a:b, :] = (mixed / total).astype(jnp.bfloat16)


def attend(scalars, blocks, gain, shift, weight, bias, order):
    rows, width = blocks[0].shape
    vm = pl.BlockSpec(memory_space=pltpu.VMEM)
    return pl.pallas_call(
        attend_kernel,
        out_shape=jax.ShapeDtypeStruct((width, rows), jnp.bfloat16),
        in_specs=[pl.BlockSpec(memory_space=pltpu.SMEM)] + [vm] * 9,
        out_specs=vm,
        scratch_shapes=[pltpu.VMEM((rows, D), jnp.bfloat16)],
    )(scalars, *blocks, gain, shift, weight, bias, order)


def spread_over_tensor(x):
    b = swap(x, 0, 2)
    a = swap(x, 0, 1)
    c = swap(b, 0, 1)
    return [x, a, b, c]


def relative(x, me, axis=0):
    return jnp.stack(
        [lax.dynamic_index_in_dim(x, jnp.bitwise_xor(me, i), axis, keepdims=False) for i in range(x.shape[axis])],
        axis=axis,
    )


def select_swap(flag, a, b):
    return jnp.where(flag, b, a), jnp.where(flag, a, b)


def place_kernel(block_width, scalars, p0, p1, p2, p3, out):
    rank = scalars[0]
    rows, total = p0.shape
    keep = lax.broadcasted_iota(jnp.int32, (rows, block_width), 0) < scalars[1]
    for m in range(total // block_width):
        upper = jnp.bitwise_xor(jnp.right_shift(rank, 2), m) * 4
        for d, piece in enumerate((p0, p1, p2, p3)):
            column = upper + jnp.bitwise_xor(jnp.bitwise_and(rank, 3), d)
            block = piece[:, m * block_width : (m + 1) * block_width]
            block = jnp.where(keep, block, jnp.zeros_like(block))
            start = pl.multiple_of(column * block_width, block_width)
            out[:, pl.ds(start, block_width)] = block


def place(scalars, pieces, block_width):
    rows, total = pieces[0].shape
    rank, live_rows = scalars
    if block_width % 128 == 0:
        vmem = pl.BlockSpec(memory_space=pltpu.VMEM)
        return pl.pallas_call(
            functools.partial(place_kernel, block_width),
            out_shape=jax.ShapeDtypeStruct((rows, 4 * total), pieces[0].dtype),
            in_specs=[pl.BlockSpec(memory_space=pltpu.SMEM)] + [vmem] * 4,
            out_specs=vmem,
        )(jnp.stack(scalars), *pieces)
    upper = total // block_width
    pieces = jnp.stack(pieces).reshape(4, rows, upper, block_width)
    pieces = relative(pieces, jnp.bitwise_and(rank, 3), 0)
    pieces = relative(pieces, jnp.right_shift(rank, 2), 2)
    mixed = jnp.transpose(pieces, (1, 2, 0, 3)).reshape(rows, 4 * total)
    keep = jnp.arange(rows, dtype=jnp.int32)[:, None] < live_rows
    return jnp.where(keep, mixed, jnp.zeros_like(mixed))


def compute(
    patches,
    counts,
    first_gain,
    first_shift,
    in_weight,
    in_bias,
    out_weight,
    out_bias,
    second_gain,
    second_shift,
    merger_weight,
    merger_bias,
):
    rank = lax.axis_index("dp")
    me = lax.axis_index("tensor")
    ranks = lax.axis_size("dp")
    groups = lax.axis_size("tensor")
    width = patches.shape[1]
    rows = TILE // MERGE
    block_width = merger_weight.shape[2]

    columns = [merger_weight]
    bit = 4
    while bit < ranks:
        columns = columns + [swap(c, bit) for c in columns]
        bit *= 2

    mine = lax.dynamic_slice_in_dim(counts, rank * SLOTS, SLOTS)
    theirs = lax.dynamic_slice_in_dim(counts, jnp.bitwise_xor(rank, 1) * SLOTS, SLOTS)
    own = mine[0] > 0
    count = jnp.where(own, mine[0], theirs[1])
    moved = swap(patches[TILE:], 1)
    shard = jnp.where(own, patches[:TILE], moved)

    source = jnp.arange(TILE, dtype=jnp.int32)
    order = (source % MERGE * rows + source // MERGE)[:, None] == source[None, :]
    heads_out = attend(
        jnp.stack([me, count]),
        spread_over_tensor(shard),
        first_gain[None],
        first_shift[None],
        jnp.transpose(in_weight, (1, 2, 0)).reshape(3 * width, D),
        in_bias.reshape(3 * width, 1),
        order.astype(jnp.bfloat16),
    )
    base = jnp.transpose(shard.reshape(rows, MERGE, width), (1, 0, 2)).reshape(TILE, width)
    base = base.astype(jnp.float32) + out_bias

    all_heads = jnp.concatenate(spread_over_tensor(heads_out), axis=0)
    out_rel = relative(out_weight.reshape(groups, width, width), me).reshape(D, width)
    residual = base + lax.dot_general(
        all_heads, out_rel, (((0,), (0,)), ((), ())), preferred_element_type=jnp.float32
    )
    stats = jnp.stack([jnp.sum(residual, axis=1), jnp.sum(residual * residual, axis=1)])
    stats = stats + swap(stats, 0, 1) + swap(stats, 0, 2) + swap(stats, 0, 3)
    row_mean = (stats[0] / D)[:, None]
    second = (stats[1] / D)[:, None]
    encoded = (residual - row_mean) * lax.rsqrt(
        second - row_mean * row_mean + EPS
    ) * second_gain + second_shift
    merged = encoded.astype(jnp.bfloat16).reshape(MERGE, rows, width)
    merged = jnp.transpose(merged, (1, 0, 2)).reshape(rows, MERGE * width)

    images = jnp.concatenate([merged] + [swap(merged, i) for i in (1, 2, 3)], axis=0)
    held = jnp.concatenate([c.reshape(MERGE * width, block_width) for c in columns], axis=1)
    total = held.shape[1]
    product = jnp.dot(images, held, preferred_element_type=jnp.float32).astype(jnp.bfloat16)

    low = jnp.bitwise_and(me, 1) == 1
    high = jnp.right_shift(me, 1) == 1
    product = product.reshape(4, 2, rows // 2, total)
    kept, sent = select_swap(low, product[:, 0], product[:, 1])
    half = kept.astype(jnp.float32) + swap(sent, 0, 1).astype(jnp.float32)
    half = half.reshape(2, 2, rows // 2, total)
    kept, sent = select_swap(high, half[:, 0], half[:, 1])
    bias = lax.dynamic_index_in_dim(
        merger_bias.reshape(ranks // 4, 4, block_width), jnp.bitwise_and(rank, 3), 1, keepdims=False
    )
    bias = relative(bias, jnp.right_shift(rank, 2)).reshape(total)
    summed = kept + swap(sent.astype(jnp.bfloat16), 0, 2).astype(jnp.float32) + bias
    summed = summed.astype(jnp.bfloat16)

    pieces = [summed[0], swap(summed[0], 1, 2), swap(summed[1], 2, 0), swap(summed[1], 3, 2)]
    slot = jnp.right_shift(me, 1)
    row_count = lax.dynamic_index_in_dim(mine, slot, 0, keepdims=False)
    first_row = jnp.bitwise_and(me, 1) * (rows // 2)
    live_rows = jnp.right_shift(row_count, 2) - first_row
    return place((rank, live_rows), pieces, block_width)


def solution(mesh):
    return jax.shard_map(
        compute,
        mesh=mesh,
        in_specs=(
            P("dp", "tensor"),
            P(),
            P(),
            P(),
            P(None, None, "tensor"),
            P(None, "tensor"),
            P(None, "tensor"),
            P("tensor"),
            P("tensor"),
            P("tensor"),
            P(None, "tensor", "dp"),
            P(),
        ),
        out_specs=P(("dp", "tensor"), None),
        check_vma=False,
    )
```

profile of v0, /device:TPU:0, one launch (start us, length us, event | category | flops | bytes accessed | tf_op | source)
XLA Modules:
  0.0 129.4 jit_solution(4607136627443439276)
XLA Ops:
  0.0 1.2 fusion.42
  1.2 0.2 copy.30
  1.4 3.1 %collective-permute-start = (bf16[512,320]{1,0:T(8,128)(2,1)S(1)}, bf16[512,320]{1,0:T(8,128)(2,1)S(1)}, u32[]{:S(2)}, u32[]{:S(2)}) collective-permute-start(bf16[512,320]{1,0:T(8,128)(2,1)S(1)} %copy.30), channel_id=1, source_target_pairs={{0,4},{1,5},{2,6},{3,7},{4,0},{5,1},{6,2},{7,3},{8,12},{9,13},{10,... | collective-permute-start | bytes 983048 | tf_op jit(solution)/shard_map/ppermute | solution.py:25
  4.6 0.2 copy.29
  4.8 8.8 %collective-permute-done = bf16[512,320]{1,0:T(8,128)(2,1)S(1)} collective-permute-done((bf16[512,320]{1,0:T(8,128)(2,1)S(1)}, bf16[512,320]{1,0:T(8,128)(2,1)S(1)}, u32[]{:S(2)}, u32[]{:S(2)}) %collective-permute-start) | collective-permute-done | bytes 327712 | tf_op jit(solution)/shard_map/ppermute | solution.py:25
  13.6 1.8 %collective-permute-start.2 = (bf16[512,320]{1,0:T(8,128)(2,1)S(1)}, bf16[512,320]{1,0:T(8,128)(2,1)S(1)}, u32[]{:S(2)}, u32[]{:S(2)}) collective-permute-start(bf16[512,320]{1,0:T(8,128)(2,1)S(1)} %broadcast_select_fusion.own), channel_id=1, source_target_pairs={{0,2},{1,3},{2,0},{3,1},{4,6},{5,7},{6,4},{7,5},{8,10},{9,11},{10,... | collective-permute-start | bytes 983048 | tf_op jit(solution)/shard_map/ppermute | solution.py:25
  15.4 0.6 slice.42
  16.7 1.1 reshape.119.bias
  17.9 0.6 broadcast_in_dim.4.gain
  18.4 0.6 broadcast_in_dim.5.shift
  19.1 4.9 %collective-permute-done.2.far = bf16[512,320]{1,0:T(8,128)(2,1)S(1)} collective-permute-done((bf16[512,320]{1,0:T(8,128)(2,1)S(1)}, bf16[512,320]{1,0:T(8,128)(2,1)S(1)}, u32[]{:S(2)}, u32[]{:S(2)}) %collective-permute-start.2) | collective-permute-done | bytes 327712 | tf_op jit(solution)/shard_map/ppermute | solution.py:25
  24.0 0.7 pad_add_fusion.1.scalars
  24.7 0.9 fusion.25.order
  25.7 0.7 copy-done.5
  26.6 8.1 %shard_map.118 = bf16[320,512]{1,0:T(8,128)(2,1)} custom-call(s32[2]{0:T(128)} %pad_add_fusion.1.scalars, bf16[512,320]{1,0:T(8,128)(2,1)} %copy-done, bf16[512,320]{1,0:T(8,128)(2,1)} %copy-done.5, bf16[512,320]{1,0:T(8,128)(2,1)} %copy-done.4, bf16[512,320]{1,0:T(8,128)(2,1)} %copy-done.6, f32[1,1280]{1,0:T(1,128)} %broadcast_in_dim.4.gain, ...), custom_call_target="tpu_custom_call" | custom-call | tf_op jit(solution)/shard_map/pallas_call | solution.py:78
  34.6 1.4 %collective-permute-start.5 = (bf16[320,512]{1,0:T(8,128)(2,1)}, bf16[320,512]{1,0:T(8,128)(2,1)S(1)}, u32[]{:S(2)}, u32[]{:S(2)}) collective-permute-start(bf16[320,512]{1,0:T(8,128)(2,1)} %shard_map.118), channel_id=1, source_target_pairs={{0,2},{1,3},{2,0},{3,1},{4,6},{5,7},{6,4},{7,5},{8,10},{9,11},{10,... | collective-permute-start | bytes 983048 | tf_op jit(solution)/shard_map/ppermute | solution.py:25
  36.1 2.6 %collective-permute-start.13 = (bf16[4,320,512]{2,1,0:T(8,128)(2,1)}, bf16[4,320,512]{2,1,0:T(8,128)(2,1)}, u32[]{:S(2)}, u32[]{:S(2)}) collective-permute-start(bf16[4,320,512]{2,1,0:T(8,128)(2,1)} %param.22), channel_id=1, source_target_pairs={{0,16},{1,17},{2,18},{3,19},{4,20},{5,21},{6,22},{7,23},{8,24},{9,... | collective-permute-start | bytes 3932168 | tf_op jit(solution)/shard_map/ppermute | solution.py:25
  38.7 1.1 reshape.107
  39.8 5.1 %collective-permute-done.5 = bf16[320,512]{1,0:T(8,128)(2,1)S(1)} collective-permute-done((bf16[320,512]{1,0:T(8,128)(2,1)}, bf16[320,512]{1,0:T(8,128)(2,1)S(1)}, u32[]{:S(2)}, u32[]{:S(2)}) %collective-permute-start.5) | collective-permute-done | bytes 327712 | tf_op jit(solution)/shard_map/ppermute | solution.py:25
  44.9 2.0 %constant_dynamic-slice_fusion.3 = (bf16[1,320,320]{1,0,2:T(2,128)(2,1)S(1)}, bf16[1,320,320]{1,0,2:T(2,128)(2,1)S(1)}, bf16[1,320,320]{1,0,2:T(2,128)(2,1)S(1)}, bf16[1,320,320]{1,0,2:T(2,128)(2,1)S(1)}) fusion(bf16[4,320,320]{1,0,2:T(4,128)(2,1)S(1)} %reshape.107, s32[]{:T(128)S(6)} %select_n.119, s32[]{:T(128)S(6)} %select_n.122, s32[]{:T(128)S(6)} %select_n.121, ...), kind=kLoop, calls=%fused_computation.67 | loop fusion | bytes 1638416 | tf_op jit(solution)/shard_map/jit(dynamic_index_in_dim)/dynamic_slice | solution.py:96
  47.0 2.5 %pad_maximum_fusion = bf16[4,320,320]{1,0,2:T(4,128)(2,1)S(1)} fusion(bf16[1,320,320]{1,0,2:T(2,128)(2,1)S(1)} %get-tuple-element.8, bf16[1,320,320]{1,0,2:T(2,128)(2,1)S(1)} %get-tuple-element.9, bf16[1,320,320]{1,0,2:T(2,128)(2,1)S(1)} %get-tuple-element.10, bf16[1,320,320]{1,0,2:T(2,128)(2,1)S(1)} %get-tuple-element.7), kind=kLoop, calls=%fused_computation.24 | loop fusion | flops 3276800 | bytes 1638400 | tf_op jit(solution)/shard_map/stack | solution.py:95
  49.4 0.9 reshape.108
  50.6 0.3 copy.22
  51.0 1.6 %fusion.41 = (f32[512]{0:T(512)S(1)}, f32[512]{0:T(512)S(1)}, f32[512,320]{0,1:T(8,128)S(1)}) fusion(bf16[1280,320]{0,1:T(8,128)(2,1)S(1)} %reshape.108, bf16[320,512]{1,0:T(8,128)(2,1)} %collective-permute-done.6, bf16[320,512]{1,0:T(8,128)(2,1)S(1)} %collective-permute-done.5, bf16[320,512]{1,0:T(8,128)(2,1)S(1)} %collective-permute-done.4, ...), kind=kOutput, calls=%fused_computation.72 | convolution fusion | flops 425491456 | bytes 3446016 | tf_op jit(solution)/shard_map/dot_general | solution.py:190
  52.6 0.6 collective-permute-start.7
  53.2 1.4 %collective-permute-start.8 = (f32[2,512]{1,0:T(2,128)S(1)}, f32[2,512]{1,0:T(2,128)S(1)}, u32[]{:S(2)}, u32[]{:S(2)}) collective-permute-start(f32[2,512]{1,0:T(2,128)S(1)} %pad_maximum_fusion.1), channel_id=1, source_target_pairs={{0,2},{1,3},{2,0},{3,1},{4,6},{5,7},{6,4},{7,5},{8,10},{9,11},{10,... | collective-permute-start | bytes 12296 | tf_op jit(solution)/shard_map/ppermute | solution.py:25
  54.6 2.2 %collective-permute-done.8 = f32[2,512]{1,0:T(2,128)S(1)} collective-permute-done((f32[2,512]{1,0:T(2,128)S(1)}, f32[2,512]{1,0:T(2,128)S(1)}, u32[]{:S(2)}, u32[]{:S(2)}) %collective-permute-start.8) | collective-permute-done | bytes 4128 | tf_op jit(solution)/shard_map/ppermute | solution.py:25
  56.8 0.9 collective-permute-done.9
  57.9 1.6 %collective-permute-start.10 = (bf16[128,1280]{0,1:T(8,128)(2,1)S(1)}, bf16[128,1280]{0,1:T(8,128)(2,1)S(1)}, u32[]{:S(2)}, u32[]{:S(2)}) collective-permute-start(bf16[128,1280]{0,1:T(8,128)(2,1)S(1)} %bitcast.99), channel_id=1, source_target_pairs={{0,4},{1,5},{2,6},{3,7},{4,0},{5,1},{6,2},{7,3},{8,12},{9,13},{10,... | collective-permute-start | bytes 983048 | tf_op jit(solution)/shard_map/ppermute | solution.py:25
  59.5 1.6 %collective-permute-start.11 = (bf16[128,1280]{0,1:T(8,128)(2,1)S(1)}, bf16[128,1280]{0,1:T(8,128)(2,1)S(1)}, u32[]{:S(2)}, u32[]{:S(2)}) collective-permute-start(bf16[128,1280]{0,1:T(8,128)(2,1)S(1)} %bitcast.100), channel_id=1, source_target_pairs={{0,8},{1,9},{2,10},{3,11},{4,12},{5,13},{6,14},{7,15},{8,0},{9,1},... | collective-permute-start | bytes 983048 | tf_op jit(solution)/shard_map/ppermute | solution.py:25
  61.1 0.4 collective-permute-start.12
  61.5 34.9 %collective-permute-done.13 = bf16[4,320,512]{2,1,0:T(8,128)(2,1)} collective-permute-done((bf16[4,320,512]{2,1,0:T(8,128)(2,1)}, bf16[4,320,512]{2,1,0:T(8,128)(2,1)}, u32[]{:S(2)}, u32[]{:S(2)}) %collective-permute-start.13) | collective-permute-done | bytes 1310752 | tf_op jit(solution)/shard_map/ppermute | solution.py:25
  96.3 0.7 collective-permute-done.11
  97.1 5.9 %collective-permute-done.12 = bf16[128,1280]{0,1:T(8,128)(2,1)S(1)} collective-permute-done((bf16[128,1280]{0,1:T(8,128)(2,1)S(1)}, bf16[128,1280]{0,1:T(8,128)(2,1)S(1)}, u32[]{:S(2)}, u32[]{:S(2)}) %collective-permute-start.12) | collective-permute-done | bytes 327712 | tf_op jit(solution)/shard_map/ppermute | solution.py:25
  103.0 3.3 %fusion.4 = bf16[512,1024]{1,0:T(8,128)(2,1)S(1)} fusion(bf16[1280,512]{1,0:T(8,128)(2,1)} %bitcast.18, bf16[1280,512]{1,0:T(8,128)(2,1)} %bitcast.113, bf16[128,1280]{0,1:T(8,128)(2,1)S(1)} %collective-permute-done.12, bf16[128,1280]{0,1:T(8,128)(2,1)S(1)} %collective-permute-done.11, bf16[128,1280]{0,1:T(8,128)(2,1)S(1)} %collective-permute-done.10, ...), kind=kOutput, calls=%fused_computation.4 | convolution fusion | flops 1353187328 | bytes 4980736 | tf_op jit(solution)/shard_map/dot_general | solution.py:206
  106.4 1.9 %collective-permute-done.14 = bf16[4,64,1024]{2,1,0:T(8,128)(2,1)S(1)} collective-permute-done((bf16[4,64,1024]{2,1,0:T(8,128)(2,1)S(1)}, bf16[4,64,1024]{2,1,0:T(8,128)(2,1)S(1)}, u32[]{:S(2)}, u32[]{:S(2)}) %collective-permute-start.14) | collective-permute-done | bytes 524320 | tf_op jit(solution)/shard_map/ppermute | solution.py:25
  108.3 0.3 convert_add_fusion
  108.6 0.7 collective-permute-start.15
  109.4 7.6 %collective-permute-done.15 = bf16[2,64,1024]{2,1,0:T(8,128)(2,1)S(1)} collective-permute-done((bf16[2,64,1024]{2,1,0:T(8,128)(2,1)S(1)}, bf16[2,64,1024]{2,1,0:T(8,128)(2,1)S(1)}, u32[]{:S(2)}, u32[]{:S(2)}) %collective-permute-start.15) | collective-permute-done | bytes 262176 | tf_op jit(solution)/shard_map/ppermute | solution.py:25
  117.2 1.7 %collective-permute-start.16 = (bf16[64,1024]{1,0:T(8,128)(2,1)S(1)}, bf16[64,1024]{1,0:T(8,128)(2,1)S(1)}, u32[]{:S(2)}, u32[]{:S(2)}) collective-permute-start(bf16[64,1024]{1,0:T(8,128)(2,1)S(1)} %get-tuple-element.14.p0), channel_id=1, source_target_pairs={{0,6},{1,7},{2,4},{3,5},{4,2},{5,3},{6,0},{7,1},{8,14},{9,15},{10,... | collective-permute-start | bytes 393224 | tf_op jit(solution)/shard_map/ppermute | solution.py:25
  118.9 2.7 %collective-permute-start.18 = (bf16[64,1024]{1,0:T(8,128)(2,1)S(1)}, bf16[64,1024]{1,0:T(8,128)(2,1)S(1)}, u32[]{:S(2)}, u32[]{:S(2)}) collective-permute-start(bf16[64,1024]{1,0:T(8,128)(2,1)S(1)} %get-tuple-element.13), channel_id=1, source_target_pairs={{0,14},{1,15},{2,12},{3,13},{4,10},{5,11},{6,8},{7,9},{8,6},{9,7},... | collective-permute-start | bytes 393224 | tf_op jit(solution)/shard_map/ppermute | solution.py:25
  121.6 0.6 dynamic_slice.39
  122.8 0.6 pad_add_fusion.scalars
  123.5 0.7 collective-permute-done.16.p1
  124.2 0.5 collective-permute-done.17.p2
  124.7 2.1 %collective-permute-done.18.p3 = bf16[64,1024]{1,0:T(8,128)(2,1)S(1)} collective-permute-done((bf16[64,1024]{1,0:T(8,128)(2,1)S(1)}, bf16[64,1024]{1,0:T(8,128)(2,1)S(1)}, u32[]{:S(2)}, u32[]{:S(2)}) %collective-permute-start.18) | collective-permute-done | bytes 131104 | tf_op jit(solution)/shard_map/ppermute | solution.py:25
  126.8 0.6 copy-done.10
  127.5 1.9 %shard_map.119 = bf16[64,4096]{1,0:T(8,128)(2,1)} custom-call(s32[2]{0:T(128)} %pad_add_fusion.scalars, bf16[64,1024]{1,0:T(8,128)(2,1)} %copy-done.3, bf16[64,1024]{1,0:T(8,128)(2,1)} %copy-done.8, bf16[64,1024]{1,0:T(8,128)(2,1)} %copy-done.9, bf16[64,1024]{1,0:T(8,128)(2,1)} %copy-done.10), custom_call_target="tpu_custom_call" | custom-call | tf_op jit(solution)/shard_map/pallas_call | solution.py:124
  (66 shorter events, 1.2 us)
Async XLA Ops:
  0.0 4.5 %copy-start.17 = (s32[16]{0:T(128)S(1)}, s32[16]{0:T(128)}, u32[]{:S(2)}) copy-start(s32[16]{0:T(128)} %param.13) | copy-start | bytes 196
  0.0 16.7 %copy-start.14 = (f32[3,320]{1,0:T(4,128)S(1)}, f32[3,320]{1,0:T(4,128)}, u32[]{:S(2)}) copy-start(f32[3,320]{1,0:T(4,128)} %param.17) | copy-start | bytes 11524
  0.0 17.9 %copy-start.12 = (f32[1280]{0:T(1024)S(1)}, f32[1280]{0:T(1024)}, u32[]{:S(2)}) copy-start(f32[1280]{0:T(1024)} %param.14) | copy-start | bytes 15364
  0.0 18.4 %copy-start.13 = (f32[1280]{0:T(1024)S(1)}, f32[1280]{0:T(1024)}, u32[]{:S(2)}) copy-start(f32[1280]{0:T(1024)} %param.15) | copy-start | bytes 15364
  1.4 12.2 %collective-permute-start = (bf16[512,320]{1,0:T(8,128)(2,1)S(1)}, bf16[512,320]{1,0:T(8,128)(2,1)S(1)}, u32[]{:S(2)}, u32[]{:S(2)}) collective-permute-start(bf16[512,320]{1,0:T(8,128)(2,1)S(1)} %copy.30), channel_id=1, source_target_pairs={{0,4},{1,5},{2,6},{3,7},{4,0},{5,1},{6,2},{7,3},{8,12},{9,13},{10,... | collective-permute-start | bytes 983048 | tf_op jit(solution)/shard_map/ppermute | solution.py:25
  13.6 12.1 %copy-start = (bf16[512,320]{1,0:T(8,128)(2,1)}, bf16[512,320]{1,0:T(8,128)(2,1)S(1)}, u32[]{:S(2)}) copy-start(bf16[512,320]{1,0:T(8,128)(2,1)S(1)} %broadcast_select_fusion.own) | copy-start | bytes 983044
  13.6 10.3 %collective-permute-start.2 = (bf16[512,320]{1,0:T(8,128)(2,1)S(1)}, bf16[512,320]{1,0:T(8,128)(2,1)S(1)}, u32[]{:S(2)}, u32[]{:S(2)}) collective-permute-start(bf16[512,320]{1,0:T(8,128)(2,1)S(1)} %broadcast_select_fusion.own), channel_id=1, source_target_pairs={{0,2},{1,3},{2,0},{3,1},{4,6},{5,7},{6,4},{7,5},{8,10},{9,11},{10,... | collective-permute-start | bytes 983048 | tf_op jit(solution)/shard_map/ppermute | solution.py:25
  19.1 6.6 %collective-permute-start.1 = (bf16[512,320]{1,0:T(8,128)(2,1)S(1)}, bf16[512,320]{1,0:T(8,128)(2,1)S(1)}, u32[]{:S(2)}, u32[]{:S(2)}) collective-permute-start(bf16[512,320]{1,0:T(8,128)(2,1)S(1)} %broadcast_select_fusion.own), channel_id=1, source_target_pairs={{0,1},{1,0},{2,3},{3,2},{4,5},{5,4},{6,7},{7,6},{8,9},{9,8},{10,11... | collective-permute-start | bytes 983048 | tf_op jit(solution)/shard_map/ppermute | solution.py:25
  24.0 1.7 %copy-start.4 = (bf16[512,320]{1,0:T(8,128)(2,1)}, bf16[512,320]{1,0:T(8,128)(2,1)S(1)}, u32[]{:S(2)}) copy-start(bf16[512,320]{1,0:T(8,128)(2,1)S(1)} %collective-permute-done.2.far) | copy-start | bytes 983044
  24.0 1.7 %collective-permute-start.3 = (bf16[512,320]{1,0:T(8,128)(2,1)S(1)}, bf16[512,320]{1,0:T(8,128)(2,1)S(1)}, u32[]{:S(2)}, u32[]{:S(2)}) collective-permute-start(bf16[512,320]{1,0:T(8,128)(2,1)S(1)} %collective-permute-done.2.far), channel_id=1, source_target_pairs={{0,1},{1,0},{2,3},{3,2},{4,5},{5,4},{6,7},{7,6},{8,9},{9,8},{10,11... | collective-permute-start | bytes 983048 | tf_op jit(solution)/shard_map/ppermute | solution.py:25
  25.7 0.8 copy-start.5
  25.7 0.9 copy-start.6
  26.6 12.1 %copy-start.2 = (bf16[1280,320]{0,1:T(8,128)(2,1)S(1)}, bf16[1280,320]{0,1:T(8,128)(2,1)}, u32[]{:S(2)}) copy-start(bf16[1280,320]{0,1:T(8,128)(2,1)} %param.18) | copy-start | bytes 2457604
  34.6 10.3 %collective-permute-start.5 = (bf16[320,512]{1,0:T(8,128)(2,1)}, bf16[320,512]{1,0:T(8,128)(2,1)S(1)}, u32[]{:S(2)}, u32[]{:S(2)}) collective-permute-start(bf16[320,512]{1,0:T(8,128)(2,1)} %shard_map.118), channel_id=1, source_target_pairs={{0,2},{1,3},{2,0},{3,1},{4,6},{5,7},{6,4},{7,5},{8,10},{9,11},{10,... | collective-permute-start | bytes 983048 | tf_op jit(solution)/shard_map/ppermute | solution.py:25
  36.1 60.3 %collective-permute-start.13 = (bf16[4,320,512]{2,1,0:T(8,128)(2,1)}, bf16[4,320,512]{2,1,0:T(8,128)(2,1)}, u32[]{:S(2)}, u32[]{:S(2)}) collective-permute-start(bf16[4,320,512]{2,1,0:T(8,128)(2,1)} %param.22), channel_id=1, source_target_pairs={{0,16},{1,17},{2,18},{3,19},{4,20},{5,21},{6,22},{7,23},{8,24},{9,... | collective-permute-start | bytes 3932168 | tf_op jit(solution)/shard_map/ppermute | solution.py:25
  39.7 11.2 %collective-permute-start.4 = (bf16[320,512]{1,0:T(8,128)(2,1)}, bf16[320,512]{1,0:T(8,128)(2,1)S(1)}, u32[]{:S(2)}, u32[]{:S(2)}) collective-permute-start(bf16[320,512]{1,0:T(8,128)(2,1)} %shard_map.118), channel_id=1, source_target_pairs={{0,1},{1,0},{2,3},{3,2},{4,5},{5,4},{6,7},{7,6},{8,9},{9,8},{10,11... | collective-permute-start | bytes 983048 | tf_op jit(solution)/shard_map/ppermute | solution.py:25
  44.9 6.0 %collective-permute-start.6 = (bf16[320,512]{1,0:T(8,128)(2,1)S(1)}, bf16[320,512]{1,0:T(8,128)(2,1)}, u32[]{:S(2)}, u32[]{:S(2)}) collective-permute-start(bf16[320,512]{1,0:T(8,128)(2,1)S(1)} %collective-permute-done.5), channel_id=1, source_target_pairs={{0,1},{1,0},{2,3},{3,2},{4,5},{5,4},{6,7},{7,6},{8,9},{9,8},{10,11... | collective-permute-start | bytes 983048 | tf_op jit(solution)/shard_map/ppermute | solution.py:25
  46.9 3.4 %copy-start.1 = (bf16[512,320]{1,0:T(8,128)(2,1)S(1)}, bf16[512,320]{1,0:T(8,128)(2,1)}, u32[]{:S(2)}) copy-start(bf16[512,320]{1,0:T(8,128)(2,1)} %copy-done) | copy-start | bytes 983044
  49.4 1.6 %copy-start.7 = (bf16[320,512]{1,0:T(8,128)(2,1)S(1)}, bf16[320,512]{1,0:T(8,128)(2,1)}, u32[]{:S(2)}) copy-start(bf16[320,512]{1,0:T(8,128)(2,1)} %shard_map.118) | copy-start | bytes 983044
  49.4 1.6 %copy-start.18 = (f32[320]{0:T(512)S(1)}, f32[320]{0:T(512)}, u32[]{:S(2)}) copy-start(f32[320]{0:T(512)} %param.19) | copy-start | bytes 3844
  51.0 6.7 %copy-start.15 = (f32[320]{0:T(512)S(1)}, f32[320]{0:T(512)}, u32[]{:S(2)}) copy-start(f32[320]{0:T(512)} %param.21) | copy-start | bytes 3844
  51.0 6.7 %copy-start.16 = (f32[320]{0:T(512)S(1)}, f32[320]{0:T(512)}, u32[]{:S(2)}) copy-start(f32[320]{0:T(512)} %param.20) | copy-start | bytes 3844
  52.6 2.0 %collective-permute-start.7 = (f32[2,512]{1,0:T(2,128)S(1)}, f32[2,512]{1,0:T(2,128)S(1)}, u32[]{:S(2)}, u32[]{:S(2)}) collective-permute-start(f32[2,512]{1,0:T(2,128)S(1)} %pad_maximum_fusion.1), channel_id=1, source_target_pairs={{0,1},{1,0},{2,3},{3,2},{4,5},{5,4},{6,7},{7,6},{8,9},{9,8},{10,11... | collective-permute-start | bytes 12296 | tf_op jit(solution)/shard_map/ppermute | solution.py:25
  53.2 3.6 %collective-permute-start.8 = (f32[2,512]{1,0:T(2,128)S(1)}, f32[2,512]{1,0:T(2,128)S(1)}, u32[]{:S(2)}, u32[]{:S(2)}) collective-permute-start(f32[2,512]{1,0:T(2,128)S(1)} %pad_maximum_fusion.1), channel_id=1, source_target_pairs={{0,2},{1,3},{2,0},{3,1},{4,6},{5,7},{6,4},{7,5},{8,10},{9,11},{10,... | collective-permute-start | bytes 12296 | tf_op jit(solution)/shard_map/ppermute | solution.py:25
  54.6 3.1 %collective-permute-start.9 = (f32[2,512]{1,0:T(2,128)S(1)}, f32[2,512]{1,0:T(2,128)S(1)}, u32[]{:S(2)}, u32[]{:S(2)}) collective-permute-start(f32[2,512]{1,0:T(2,128)S(1)} %pad_maximum_fusion.1), channel_id=1, source_target_pairs={{0,3},{1,2},{2,1},{3,0},{4,7},{5,6},{6,5},{7,4},{8,11},{9,10},{10,... | collective-permute-start | bytes 12296 | tf_op jit(solution)/shard_map/ppermute | solution.py:25
  57.9 38.4 %collective-permute-start.10 = (bf16[128,1280]{0,1:T(8,128)(2,1)S(1)}, bf16[128,1280]{0,1:T(8,128)(2,1)S(1)}, u32[]{:S(2)}, u32[]{:S(2)}) collective-permute-start(bf16[128,1280]{0,1:T(8,128)(2,1)S(1)} %bitcast.99), channel_id=1, source_target_pairs={{0,4},{1,5},{2,6},{3,7},{4,0},{5,1},{6,2},{7,3},{8,12},{9,13},{10,... | collective-permute-start | bytes 983048 | tf_op jit(solution)/shard_map/ppermute | solution.py:25
  59.5 37.6 %collective-permute-start.11 = (bf16[128,1280]{0,1:T(8,128)(2,1)S(1)}, bf16[128,1280]{0,1:T(8,128)(2,1)S(1)}, u32[]{:S(2)}, u32[]{:S(2)}) collective-permute-start(bf16[128,1280]{0,1:T(8,128)(2,1)S(1)} %bitcast.100), channel_id=1, source_target_pairs={{0,8},{1,9},{2,10},{3,11},{4,12},{5,13},{6,14},{7,15},{8,0},{9,1},... | collective-permute-start | bytes 983048 | tf_op jit(solution)/shard_map/ppermute | solution.py:25
  61.1 41.9 %collective-permute-start.12 = (bf16[128,1280]{0,1:T(8,128)(2,1)S(1)}, bf16[128,1280]{0,1:T(8,128)(2,1)S(1)}, u32[]{:S(2)}, u32[]{:S(2)}) collective-permute-start(bf16[128,1280]{0,1:T(8,128)(2,1)S(1)} %bitcast.101), channel_id=1, source_target_pairs={{0,12},{1,13},{2,14},{3,15},{4,8},{5,9},{6,10},{7,11},{8,4},{9,5},... | collective-permute-start | bytes 983048 | tf_op jit(solution)/shard_map/ppermute | solution.py:25
  106.3 3.0 %copy-start.11 = (f32[4096]{0:T(1024)S(1)}, f32[4096]{0:T(1024)}, u32[]{:S(2)}) copy-start(f32[4096]{0:T(1024)} %param.23) | copy-start | bytes 49156
  106.3 2.0 %collective-permute-start.14 = (bf16[4,64,1024]{2,1,0:T(8,128)(2,1)S(1)}, bf16[4,64,1024]{2,1,0:T(8,128)(2,1)S(1)}, u32[]{:S(2)}, u32[]{:S(2)}) collective-permute-start(bf16[4,64,1024]{2,1,0:T(8,128)(2,1)S(1)} %select_bitcast_fusion), channel_id=1, source_target_pairs={{0,1},{1,0},{2,3},{3,2},{4,5},{5,4},{6,7},{7,6},{8,9},{9,8},{10,11... | collective-permute-start | bytes 1572872 | tf_op jit(solution)/shard_map/ppermute | solution.py:25
  108.6 8.4 %collective-permute-start.15 = (bf16[2,64,1024]{2,1,0:T(8,128)(2,1)S(1)}, bf16[2,64,1024]{2,1,0:T(8,128)(2,1)S(1)}, u32[]{:S(2)}, u32[]{:S(2)}) collective-permute-start(bf16[2,64,1024]{2,1,0:T(8,128)(2,1)S(1)} %fusion.29), channel_id=1, source_target_pairs={{0,2},{1,3},{2,0},{3,1},{4,6},{5,7},{6,4},{7,5},{8,10},{9,11},{10,... | collective-permute-start | bytes 786440 | tf_op jit(solution)/shard_map/ppermute | solution.py:25
  117.2 9.7 %copy-start.3 = (bf16[64,1024]{1,0:T(8,128)(2,1)}, bf16[64,1024]{1,0:T(8,128)(2,1)S(1)}, u32[]{:S(2)}) copy-start(bf16[64,1024]{1,0:T(8,128)(2,1)S(1)} %get-tuple-element.14.p0) | copy-start | bytes 393220
  117.2 7.0 %collective-permute-start.16 = (bf16[64,1024]{1,0:T(8,128)(2,1)S(1)}, bf16[64,1024]{1,0:T(8,128)(2,1)S(1)}, u32[]{:S(2)}, u32[]{:S(2)}) collective-permute-start(bf16[64,1024]{1,0:T(8,128)(2,1)S(1)} %get-tuple-element.14.p0), channel_id=1, source_target_pairs={{0,6},{1,7},{2,4},{3,5},{4,2},{5,3},{6,0},{7,1},{8,14},{9,15},{10,... | collective-permute-start | bytes 393224 | tf_op jit(solution)/shard_map/ppermute | solution.py:25
  118.9 5.8 %collective-permute-start.17 = (bf16[64,1024]{1,0:T(8,128)(2,1)S(1)}, bf16[64,1024]{1,0:T(8,128)(2,1)S(1)}, u32[]{:S(2)}, u32[]{:S(2)}) collective-permute-start(bf16[64,1024]{1,0:T(8,128)(2,1)S(1)} %get-tuple-element.13), channel_id=1, source_target_pairs={{0,8},{1,9},{2,10},{3,11},{4,12},{5,13},{6,14},{7,15},{8,0},{9,1},... | collective-permute-start | bytes 393224 | tf_op jit(solution)/shard_map/ppermute | solution.py:25
  118.9 7.9 %collective-permute-start.18 = (bf16[64,1024]{1,0:T(8,128)(2,1)S(1)}, bf16[64,1024]{1,0:T(8,128)(2,1)S(1)}, u32[]{:S(2)}, u32[]{:S(2)}) collective-permute-start(bf16[64,1024]{1,0:T(8,128)(2,1)S(1)} %get-tuple-element.13), channel_id=1, source_target_pairs={{0,14},{1,15},{2,12},{3,13},{4,10},{5,11},{6,8},{7,9},{8,6},{9,7},... | collective-permute-start | bytes 393224 | tf_op jit(solution)/shard_map/ppermute | solution.py:25
  124.2 2.6 %copy-start.8 = (bf16[64,1024]{1,0:T(8,128)(2,1)}, bf16[64,1024]{1,0:T(8,128)(2,1)S(1)}, u32[]{:S(2)}) copy-start(bf16[64,1024]{1,0:T(8,128)(2,1)S(1)} %collective-permute-done.16.p1) | copy-start | bytes 393220
  124.7 2.1 %copy-start.9 = (bf16[64,1024]{1,0:T(8,128)(2,1)}, bf16[64,1024]{1,0:T(8,128)(2,1)S(1)}, u32[]{:S(2)}) copy-start(bf16[64,1024]{1,0:T(8,128)(2,1)S(1)} %collective-permute-done.17.p2) | copy-start | bytes 393220
  126.8 0.6 copy-start.10
where the time goes:
time: 130 us; the launch traced here: 129 us
  waiting for transfers between devices  76.2 us (59%)
  starting transfers between devices  19.8 us (15%)
  local copies, waits for them, and re-layouts  11.3 us (9%)
  Pallas kernels  10 us (8%)
  other arithmetic  5.5 us (4%)
  matrix products  4.86 us (4%)
  between operations  1.76 us (1%)
    ppermute x19, waiting for transfers between devices, swap(): lax.ppermute(x, ('dp', 'tensor'), [(i, i ^ flip) for i in range(total)])  76.2 us
    ppermute x19, starting transfers between devices, swap(): lax.ppermute(x, ('dp', 'tensor'), [(i, i ^ flip) for i in range(total)])  19.8 us
    pallas_call x1, Pallas kernels, attend(): pl.pallas_call(attend_kernel, out_shape=jax.ShapeDtypeStruct((width, rows...  8.05 us
    dot_general x1, matrix products, compute(): jnp.dot(images, held, preferred_element_type=jnp.float32)  3.27 us
  transfers between devices with their start and end apart: 19, of which 13 were waited for; matrix products, arithmetic and copies ran while one was open for 12% of the time, Pallas kernels for 0%

commit v1 on v0

v1 whole, which is shorter than its diff:
```python
import functools
import math

import jax
import jax.numpy as jnp
from jax import lax
from jax.experimental import pallas as pl
from jax.experimental.pallas import tpu as pltpu
from jax.sharding import PartitionSpec as P

D = 1280
HEADS = 16
TILE = 512
SLOTS = 2
MERGE = 4
LANES = 128

EPS = 1e-06
MASKED = -1e30


VMEM = pl.BlockSpec(memory_space=pltpu.VMEM)
SMEM = pl.BlockSpec(memory_space=pltpu.SMEM)


def swap(x, dp_flip=0, tensor_flip=0):
    width = lax.axis_size("tensor")
    total = lax.axis_size("dp") * width
    flip = dp_flip * width + tensor_flip
    return lax.ppermute(x, ("dp", "tensor"), [(i, i ^ flip) for i in range(total)])


def spread_over_tensor(x):
    far = swap(x, 0, 2)
    return [x, swap(x, 0, 1), far, swap(far, 0, 1)]


def relative(x, me, axis=0):
    return jnp.stack(
        [
            lax.dynamic_index_in_dim(x, jnp.bitwise_xor(me, i), axis, keepdims=False)
            for i in range(x.shape[axis])
        ],
        axis=axis,
    )


def reorder(me, blocks):
    p, q, r, s = blocks
    odd = jnp.bitwise_and(me, 1) == 1
    upper = jnp.bitwise_and(me, 2) == 2
    p, q, r, s = jnp.where(odd, q, p), jnp.where(odd, p, q), jnp.where(odd, s, r), jnp.where(odd, r, s)
    return [
        jnp.where(upper, r, p),
        jnp.where(upper, s, q),
        jnp.where(upper, p, r),
        jnp.where(upper, q, s),
    ]


def near_core(x):
    return pltpu.with_memory_space_constraint(x, pltpu.VMEM)


def attend_kernel(scalars, own, near, far, cross, vectors, weight, order, out, normed, projected, columns):
    me = scalars[0]
    count = scalars[1]
    width, rows = own.shape
    size = D // HEADS
    blocks = (own, near, far, cross)
    columns[...] = jnp.transpose(vectors[...])
    step = 32
    total = jnp.zeros((8, rows), jnp.float32)
    for r in blocks:
        for start in range(0, width, step):
            x = r[start : start + step, :].astype(jnp.float32)
            for i in range(0, step, 8):
                total += x[i : i + 8]
    mean = jnp.sum(total, axis=0, keepdims=True) / D
    total = jnp.zeros((8, rows), jnp.float32)
    for r in blocks:
        for start in range(0, width, step):
            x = r[start : start + step, :].astype(jnp.float32) - mean
            x = x * x
            for i in range(0, step, 8):
                total += x[i : i + 8]
    inverse = lax.rsqrt(jnp.sum(total, axis=0, keepdims=True) / D + EPS)
    for i, r in enumerate(blocks):
        first = jnp.bitwise_xor(me, i) * width
        for start in range(0, width, step):
            part = pl.ds(pl.multiple_of(first + start, step), step)
            line = (r[start : start + step, :].astype(jnp.float32) - mean) * inverse
            normed[part, :] = (line * columns[part, 0:1] + columns[part, 1:2]).astype(jnp.bfloat16)
    scale = math.log2(math.e) / math.sqrt(size)
    for p in range(3):
        part = slice(p * width, (p + 1) * width)
        got = jnp.dot(weight[part, :], normed[...], preferred_element_type=jnp.float32) + columns[part, 2:3]
        projected[part, :] = (got * scale if p == 0 else got).astype(jnp.bfloat16)
    queries = jnp.dot(projected[:width, :], order[...], preferred_element_type=jnp.float32)
    projected[:width, :] = queries.astype(jnp.bfloat16)
    place = lax.broadcasted_iota(jnp.int32, (16, rows), 1)
    first = lax.broadcasted_iota(jnp.int32, (16, rows), 0) == 0
    dead = jnp.where((place >= count) & first, MASKED, 0.0).astype(jnp.bfloat16)
    ones = jnp.ones((16, rows), jnp.bfloat16)
    for h in range(width // size):
        part = slice(h * size, (h + 1) * size)
        queries = jnp.concatenate([projected[part, :], ones], axis=0)
        keys = projected[width + h * size : width + (h + 1) * size, :]
        keys = jnp.concatenate([keys, dead], axis=0)
        values = projected[2 * width + h * size : 2 * width + (h + 1) * size, :]
        for c in range(0, rows, 256):
            scores = lax.dot_general(
                keys, queries[:, c : c + 256], (((0,), (0,)), ((), ())), preferred_element_type=jnp.float32
            )
            raised = jnp.exp2(scores - jnp.max(scores, axis=0, keepdims=True))
            total = jnp.sum(raised, axis=0, keepdims=True)
            mixed = jnp.dot(values, raised.astype(jnp.bfloat16), preferred_element_type=jnp.float32)
            out[part, c : c + 256] = (mixed / total).astype(jnp.bfloat16)


def attend(scalars, blocks, vectors, weight, order):
    width, rows = blocks[0].shape
    operands = [near_core(x) for x in (*blocks, vectors, staged(weight), order)]
    return pl.pallas_call(
        attend_kernel,
        out_shape=pltpu.VMEM((width, rows), jnp.bfloat16),
        in_specs=[SMEM] + [VMEM] * 7,
        out_specs=VMEM,
        scratch_shapes=[
            pltpu.VMEM((D, rows), jnp.bfloat16),
            pltpu.VMEM((3 * width, rows), jnp.bfloat16),
            pltpu.VMEM((D, vectors.shape[0]), jnp.float32),
        ],
        compiler_params=pltpu.CompilerParams(vmem_limit_bytes=20 << 20),
    )(scalars, *operands)


def stage_kernel(source, out):
    pltpu.sync_copy(source, out)


def staged(x):
    return pl.pallas_call(
        stage_kernel,
        out_shape=pltpu.VMEM(x.shape, x.dtype),
        in_specs=[pl.BlockSpec(memory_space=pl.ANY)],
        out_specs=VMEM,
        compiler_params=pltpu.CompilerParams(vmem_limit_bytes=8 << 20),
    )(x)


def place_kernel(block_width, scalars, p0, p1, p2, p3, out):
    rank = scalars[0]
    rows, total = p0.shape
    keep = lax.broadcasted_iota(jnp.int32, (rows, block_width), 0) < scalars[1]
    for m in range(total // block_width):
        upper = jnp.bitwise_xor(jnp.right_shift(rank, 2), m) * 4
        for d, piece in enumerate((p0, p1, p2, p3)):
            column = upper + jnp.bitwise_xor(jnp.bitwise_and(rank, 3), d)
            block = piece[:, m * block_width : (m + 1) * block_width]
            block = jnp.where(keep, block, jnp.zeros_like(block))
            start = pl.multiple_of(column * block_width, block_width)
            out[:, pl.ds(start, block_width)] = block


def place(scalars, pieces, block_width):
    rows, total = pieces[0].shape
    rank, live_rows = scalars
    if block_width % LANES == 0:
        return pl.pallas_call(
            functools.partial(place_kernel, block_width),
            out_shape=jax.ShapeDtypeStruct((rows, 4 * total), pieces[0].dtype),
            in_specs=[SMEM] + [VMEM] * 4,
            out_specs=VMEM,
            compiler_params=pltpu.CompilerParams(vmem_limit_bytes=12 << 20),
        )(jnp.stack(scalars), *[near_core(x) for x in pieces])
    upper = total // block_width
    pieces = jnp.stack(pieces).reshape(4, rows, upper, block_width)
    pieces = relative(pieces, jnp.bitwise_and(rank, 3), 0)
    pieces = relative(pieces, jnp.right_shift(rank, 2), 2)
    mixed = jnp.transpose(pieces, (1, 2, 0, 3)).reshape(rows, 4 * total)
    keep = jnp.arange(rows, dtype=jnp.int32)[:, None] < live_rows
    return jnp.where(keep, mixed, jnp.zeros_like(mixed))


def compute(
    patches,
    counts,
    first_gain,
    first_shift,
    in_weight,
    in_bias,
    out_weight,
    out_bias,
    second_gain,
    second_shift,
    merger_weight,
    merger_bias,
):
    rank = lax.axis_index("dp")
    me = lax.axis_index("tensor")
    ranks = lax.axis_size("dp")
    width = patches.shape[1]
    rows = TILE // MERGE
    block_width = merger_weight.shape[2]

    features = jnp.transpose(patches)

    mine = lax.dynamic_slice_in_dim(counts, rank * SLOTS, SLOTS)
    theirs = lax.dynamic_slice_in_dim(counts, jnp.bitwise_xor(rank, 1) * SLOTS, SLOTS)
    own = mine[0] > 0
    count = jnp.where(own, mine[0], theirs[1])
    moved = swap(features[:, TILE:], 1)
    shard = jnp.where(own, lax.optimization_barrier(features[:, :TILE]), moved)
    scalars = jnp.stack([me, count])

    columns = [merger_weight]
    bit = 4
    while bit < ranks:
        columns = columns + [swap(c, bit) for c in columns]
        bit *= 2
    held = jnp.concatenate([c.reshape(MERGE * width, block_width) for c in columns], axis=1)

    source = jnp.arange(TILE, dtype=jnp.int32)
    order = (source % MERGE * rows + source // MERGE)[:, None] == source[None, :]
    order = order.astype(jnp.bfloat16)
    vectors = [first_gain, first_shift, jnp.pad(in_bias.reshape(3 * width), (0, D - 3 * width))]
    vectors = jnp.pad(jnp.stack(vectors), ((0, 5), (0, 0)))
    heads_out = attend(
        scalars,
        spread_over_tensor(shard),
        vectors,
        jnp.transpose(in_weight, (1, 2, 0)).reshape(3 * width, D),
        order,
    )
    base = jnp.dot(shard, order, preferred_element_type=jnp.float32) + out_bias[:, None]
    all_heads = jnp.concatenate(reorder(me, spread_over_tensor(heads_out)), axis=0)
    residual = base + jnp.dot(
        jnp.transpose(out_weight), all_heads, preferred_element_type=jnp.float32
    )
    stats = jnp.stack([jnp.sum(residual, axis=0), jnp.sum(residual * residual, axis=0)])
    stats = stats + swap(stats, 0, 1) + swap(stats, 0, 2) + swap(stats, 0, 3)
    row_mean = stats[0] / D
    second = stats[1] / D
    encoded = (residual - row_mean) * lax.rsqrt(
        second - row_mean * row_mean + EPS
    ) * second_gain[:, None] + second_shift[:, None]
    merged = encoded.astype(jnp.bfloat16).reshape(width, MERGE, rows)
    merged = jnp.transpose(merged, (1, 0, 2)).reshape(MERGE * width, rows)

    one = swap(merged, 1)
    two = swap(merged, 2)
    cut = MERGE * width // 2
    three = swap(two[:cut], 1)
    three = jnp.concatenate([three, swap(one[cut:], 2)], axis=0)

    high = jnp.right_shift(me, 1) == 1
    bias = lax.dynamic_index_in_dim(
        merger_bias.reshape(ranks // 4, 4, block_width), jnp.bitwise_and(rank, 3), 1, keepdims=False
    )
    bias = relative(bias, jnp.right_shift(rank, 2)).reshape(ranks // 4 * block_width)

    low = jnp.bitwise_and(me, 1) == 1

    def reduced(first, second, before=None):
        lines = jnp.concatenate([first, second], axis=1)
        product = lax.dot_general(
            lines, held, (((0,), (0,)), ((), ())), preferred_element_type=jnp.float32
        ).reshape(2, 2, rows // 2, held.shape[1])
        sent = jnp.where(low, product[:, 0], product[:, 1]).astype(jnp.bfloat16)
        kept = jnp.where(low, product[:, 1], product[:, 0])
        half = kept + swap(sent, 0, 1).astype(jnp.float32)
        kept = jnp.where(high, half[1], half[0])
        sent = jnp.where(high, half[0], half[1]).astype(jnp.bfloat16)
        if before is not None:
            sent, before = lax.optimization_barrier((sent, before))
        other = swap(sent, 0, 2)
        total = kept + other.astype(jnp.float32)
        return (total + bias).astype(jnp.bfloat16), before

    near, _ = reduced(merged, one)
    pair, near = reduced(two, three, near)
    pieces = [near, swap(near, 1, 2)]
    pieces += [swap(pair, 2, 0), swap(pair, 3, 2)]

    slot = jnp.right_shift(me, 1)
    row_count = lax.dynamic_index_in_dim(mine, slot, 0, keepdims=False)
    first_row = jnp.bitwise_and(me, 1) * (rows // 2)
    live_rows = jnp.right_shift(row_count, 2) - first_row
    return place((rank, live_rows), pieces, block_width)


def solution(mesh):
    return jax.shard_map(
        compute,
        mesh=mesh,
        in_specs=(
            P("dp", "tensor"),
            P(),
            P(),
            P(),
            P(None, None, "tensor"),
            P(None, "tensor"),
            P(None, "tensor"),
            P("tensor"),
            P("tensor"),
            P("tensor"),
            P(None, "tensor", "dp"),
            P(),
        ),
        out_specs=P(("dp", "tensor"), None),
        check_vma=False,
    )
```

time: 130 us -> 130 us (level)
  starting transfers between devices: 19.8 us -> 26.5 us
  local copies, waits for them, and re-layouts: 11.3 us -> 5.63 us
  other arithmetic: 5.5 us -> 3.08 us
  matrix products: 4.86 us -> 6.37 us
    ppermute x19 -> x22, starting transfers between devices: 19.8 us -> 26.5 us  [swap(): lax.ppermute(x, ('dp', 'tensor'), [(i, i ^ flip) for i in range(total)])]
    another operation x3, other arithmetic: 3.18 us -> 0.11 us  [the longest x1 0.07 us: compute(): scalars = jnp.stack([me, count])]
    reshape x3 -> x1, local copies, waits for them, and re-layouts: 3.14 us -> 0.08 us  [compute(): in_bias.reshape(3 * width)]
    dynamic_slice x2 -> x1, local copies, waits for them, and re-layouts: 2.04 us -> 0.01 us  [relative(): lax.dynamic_index_in_dim(x, jnp.bitwise_xor(me, i), axis, keepdims=False)]
    select_n x2, other arithmetic: 0.11 us -> 2.1 us  [the longest x1 1.09 us: reorder(): jnp.where(upper, r, p)]
    dot_general x2 -> x4, matrix products: 4.86 us -> 6.37 us  [the longest x2 4.35 us: reduced(): lax.dot_general(lines, held, (((0,), (0,)), ((), ())), preferred_element_...]
    ppermute x19 -> x22, waiting for transfers between devices: 76.2 us -> 77.2 us  [swap(): lax.ppermute(x, ('dp', 'tensor'), [(i, i ^ flip) for i in range(total)])]
    pallas_call x1 -> x2, Pallas kernels: 8.05 us -> 7.7 us  [the longest x1 7.41 us: attend(): pl.pallas_call(attend_kernel, out_shape=pltpu.VMEM((width, rows), jnp.bfl...]
  transfers between devices with their start and end apart: 19 -> 22, of which waited for: 13 -> 12; matrix products, arithmetic and copies ran while one was open for 12% -> 7% of each run, Pallas kernels for 0% -> 0%
where the time goes in v1:
time: 130 us
  waiting for transfers between devices  77.2 us (59%)
  starting transfers between devices  26.5 us (20%)
  Pallas kernels  9.08 us (7%)
  matrix products  6.37 us (5%)
  local copies, waits for them, and re-layouts  5.63 us (4%)
  other arithmetic  3.08 us (2%)
  between operations  1.77 us (1%)
    ppermute x22, waiting for transfers between devices, swap(): lax.ppermute(x, ('dp', 'tensor'), [(i, i ^ flip) for i in range(total)])  77.2 us
    ppermute x22, starting transfers between devices, swap(): lax.ppermute(x, ('dp', 'tensor'), [(i, i ^ flip) for i in range(total)])  26.5 us
    pallas_call x1, Pallas kernels, attend(): pl.pallas_call(attend_kernel, out_shape=pltpu.VMEM((width, rows), jnp.bfl...  7.41 us
    dot_general x2, matrix products, reduced(): lax.dot_general(lines, held, (((0,), (0,)), ((), ())), preferred_element_...  4.35 us
  transfers between devices with their start and end apart: 22, of which 12 were waited for; matrix products, arithmetic and copies ran while one was open for 7% of the time, Pallas kernels for 0%

profile of v1, /device:TPU:0, one launch (start us, length us, event | category | flops | bytes accessed | tf_op | source)
XLA Modules:
  0.0 129.7 jit_solution(7915318475142753870)
XLA Ops:
  0.0 2.0 %fusion.49 = (bf16[320,512]{1,0:T(8,128)(2,1)}, bf16[320,512]{1,0:T(8,128)(2,1)}) fusion(bf16[320,1024]{1,0:T(8,128)(2,1)} %bitcast.102), kind=kLoop, calls=%fused_computation.89 | loop fusion | bytes 1310720 | tf_op jit(solution)/shard_map/slice | solution.py:213
  2.0 3.0 %collective-permute-start = (bf16[320,512]{1,0:T(8,128)(2,1)}, bf16[320,512]{1,0:T(8,128)(2,1)}, u32[]{:S(2)}, u32[]{:S(2)}) collective-permute-start(bf16[320,512]{1,0:T(8,128)(2,1)} %get-tuple-element.15), channel_id=1, source_target_pairs={{0,4},{1,5},{2,6},{3,7},{4,0},{5,1},{6,2},{7,3},{8,12},{9,13},{10,... | collective-permute-start | bytes 983048 | tf_op jit(solution)/shard_map/ppermute | solution.py:30
  5.0 0.1 fusion.50
  5.2 0.7 slice.60
  5.8 1.7 %copy-done.1 = bf16[1280,3,320]{0,2,1:T(8,128)(2,1)S(1)} copy-done((bf16[1280,3,320]{0,2,1:T(8,128)(2,1)S(1)}, bf16[1280,3,320]{0,2,1:T(8,128)(2,1)}, u32[]{:S(2)}) %copy-start.1) | copy-done | bytes 2457624
  7.5 0.3 shard_map.118.weight
  7.8 0.4 copy-done.6
  8.2 0.1 reshape.77
  9.1 4.0 %collective-permute-done = bf16[320,512]{1,0:T(8,128)(2,1)} collective-permute-done((bf16[320,512]{1,0:T(8,128)(2,1)}, bf16[320,512]{1,0:T(8,128)(2,1)}, u32[]{:S(2)}, u32[]{:S(2)}) %collective-permute-start) | collective-permute-done | bytes 327712 | tf_op jit(solution)/shard_map/ppermute | solution.py:30
  13.1 1.0 broadcast_select_fusion.8.own
  14.1 1.8 %collective-permute-start.2 = (bf16[320,512]{1,0:T(8,128)(2,1)S(1)}, bf16[320,512]{1,0:T(8,128)(2,1)S(1)}, u32[]{:S(2)}, u32[]{:S(2)}) collective-permute-start(bf16[320,512]{1,0:T(8,128)(2,1)S(1)} %broadcast_select_fusion.8.own), channel_id=1, source_target_pairs={{0,2},{1,3},{2,0},{3,1},{4,6},{5,7},{6,4},{7,5},{8,10},{9,11},{10,... | collective-permute-start | bytes 983048 | tf_op jit(solution)/shard_map/ppermute | solution.py:30
  16.0 7.0 %collective-permute-done.2.far = bf16[320,512]{1,0:T(8,128)(2,1)S(1)} collective-permute-done((bf16[320,512]{1,0:T(8,128)(2,1)S(1)}, bf16[320,512]{1,0:T(8,128)(2,1)S(1)}, u32[]{:S(2)}, u32[]{:S(2)}) %collective-permute-start.2) | collective-permute-done | bytes 327712 | tf_op jit(solution)/shard_map/ppermute | solution.py:30
  23.1 0.2 fusion.16.order
  23.3 1.4 %collective-permute-done.3.cross = bf16[320,512]{1,0:T(8,128)(2,1)S(1)} collective-permute-done((bf16[320,512]{1,0:T(8,128)(2,1)S(1)}, bf16[320,512]{1,0:T(8,128)(2,1)S(1)}, u32[]{:S(2)}, u32[]{:S(2)}) %collective-permute-start.3) | collective-permute-done | bytes 327712 | tf_op jit(solution)/shard_map/ppermute | solution.py:30
  24.7 7.4 %shard_map.119 = bf16[320,512]{1,0:T(8,128)(2,1)} custom-call(s32[2]{0:T(128)S(1)} %pad_add_fusion.1.scalars, bf16[320,512]{1,0:T(8,128)(2,1)S(1)} %broadcast_select_fusion.8.own, bf16[320,512]{1,0:T(8,128)(2,1)S(1)} %collective-permute-done.1.near, bf16[320,512]{1,0:T(8,128)(2,1)S(1)} %collective-permute-done.2.far, ...), custom_call_target="tpu_custom_call" | custom-call | tf_op jit(solution)/shard_map/pallas_call | solution.py:124
  32.1 1.4 %collective-permute-start.4 = (bf16[320,512]{1,0:T(8,128)(2,1)}, bf16[320,512]{1,0:T(8,128)(2,1)S(1)}, u32[]{:S(2)}, u32[]{:S(2)}) collective-permute-start(bf16[320,512]{1,0:T(8,128)(2,1)} %shard_map.119), channel_id=1, source_target_pairs={{0,2},{1,3},{2,0},{3,1},{4,6},{5,7},{6,4},{7,5},{8,10},{9,11},{10,... | collective-permute-start | bytes 983048 | tf_op jit(solution)/shard_map/ppermute | solution.py:30
  33.5 8.5 %collective-permute-done.4 = bf16[320,512]{1,0:T(8,128)(2,1)S(1)} collective-permute-done((bf16[320,512]{1,0:T(8,128)(2,1)}, bf16[320,512]{1,0:T(8,128)(2,1)S(1)}, u32[]{:S(2)}, u32[]{:S(2)}) %collective-permute-start.4) | collective-permute-done | bytes 327712 | tf_op jit(solution)/shard_map/ppermute | solution.py:30
  42.0 2.5 %collective-permute-start.14 = (bf16[4,320,512]{2,1,0:T(8,128)(2,1)}, bf16[4,320,512]{2,1,0:T(8,128)(2,1)S(1)}, u32[]{:S(2)}, u32[]{:S(2)}) collective-permute-start(bf16[4,320,512]{2,1,0:T(8,128)(2,1)} %param.22), channel_id=1, source_target_pairs={{0,16},{1,17},{2,18},{3,19},{4,20},{5,21},{6,22},{7,23},{8,24},{9,... | collective-permute-start | bytes 3932168 | tf_op jit(solution)/shard_map/ppermute | solution.py:30
  44.6 1.4 %convolution_add_fusion = f32[320,512]{1,0:T(8,128)S(1)} fusion(bf16[320,512]{1,0:T(8,128)(2,1)} %copy-done.2, s32[512]{0:T(512)S(1)} %fusion.39, f32[320]{0:T(512)S(1)} %copy-done.10), kind=kOutput, calls=%fused_computation.12 | convolution fusion | flops 168198144 | bytes 986368 | tf_op jit(solution)/shard_map/dot_general | solution.py:236
  46.0 1.1 broadcast_select_fusion.7
  47.2 0.6 fusion.48
  47.8 0.3 collective-permute-start.7
  48.1 1.5 %collective-permute-start.8 = (f32[2,512]{1,0:T(2,128)S(1)}, f32[2,512]{1,0:T(2,128)S(1)}, u32[]{:S(2)}, u32[]{:S(2)}) collective-permute-start(f32[2,512]{1,0:T(2,128)S(1)} %pad_maximum_fusion.3), channel_id=1, source_target_pairs={{0,2},{1,3},{2,0},{3,1},{4,6},{5,7},{6,4},{7,5},{8,10},{9,11},{10,... | collective-permute-start | bytes 12296 | tf_op jit(solution)/shard_map/ppermute | solution.py:30
  49.6 0.1 collective-permute-start.9
  49.7 2.0 %collective-permute-done.8 = f32[2,512]{1,0:T(2,128)S(1)} collective-permute-done((f32[2,512]{1,0:T(2,128)S(1)}, f32[2,512]{1,0:T(2,128)S(1)}, u32[]{:S(2)}, u32[]{:S(2)}) %collective-permute-start.8) | collective-permute-done | bytes 4128 | tf_op jit(solution)/shard_map/ppermute | solution.py:30
  51.7 0.9 collective-permute-done.9
  52.7 0.2 copy_bitcast_fusion
  52.8 1.6 %collective-permute-start.10 = (bf16[1280,128]{1,0:T(8,128)(2,1)S(1)}, bf16[1280,128]{1,0:T(8,128)(2,1)S(1)}, u32[]{:S(2)}, u32[]{:S(2)}) collective-permute-start(bf16[1280,128]{1,0:T(8,128)(2,1)S(1)} %bitcast.103), channel_id=1, source_target_pairs={{0,8},{1,9},{2,10},{3,11},{4,12},{5,13},{6,14},{7,15},{8,0},{9,1},... | collective-permute-start | bytes 983048 | tf_op jit(solution)/shard_map/ppermute | solution.py:30
  54.5 1.5 %collective-permute-start.12 = (bf16[1280,128]{1,0:T(8,128)(2,1)S(1)}, bf16[1280,128]{1,0:T(8,128)(2,1)S(1)}, u32[]{:S(2)}, u32[]{:S(2)}) collective-permute-start(bf16[1280,128]{1,0:T(8,128)(2,1)S(1)} %bitcast.104), channel_id=1, source_target_pairs={{0,4},{1,5},{2,6},{3,7},{4,0},{5,1},{6,2},{7,3},{8,12},{9,13},{10,... | collective-permute-start | bytes 983048 | tf_op jit(solution)/shard_map/ppermute | solution.py:30
  56.0 24.5 %collective-permute-done.10 = bf16[1280,128]{1,0:T(8,128)(2,1)S(1)} collective-permute-done((bf16[1280,128]{1,0:T(8,128)(2,1)S(1)}, bf16[1280,128]{1,0:T(8,128)(2,1)S(1)}, u32[]{:S(2)}, u32[]{:S(2)}) %collective-permute-start.10) | collective-permute-done | bytes 327712 | tf_op jit(solution)/shard_map/ppermute | solution.py:30
  80.6 1.6 %collective-permute-start.11 = (bf16[640,128]{1,0:T(8,128)(2,1)S(1)}, bf16[640,128]{1,0:T(8,128)(2,1)S(1)}, u32[]{:S(2)}, u32[]{:S(2)}) collective-permute-start(bf16[640,128]{1,0:T(8,128)(2,1)S(1)} %slice.77), channel_id=1, source_target_pairs={{0,4},{1,5},{2,6},{3,7},{4,0},{5,1},{6,2},{7,3},{8,12},{9,13},{10,... | collective-permute-start | bytes 491528 | tf_op jit(solution)/shard_map/ppermute | solution.py:30
  82.2 2.5 %collective-permute-start.13 = (bf16[640,128]{1,0:T(8,128)(2,1)S(1)}, bf16[640,128]{1,0:T(8,128)(2,1)S(1)}, u32[]{:S(2)}, u32[]{:S(2)}) collective-permute-start(bf16[640,128]{1,0:T(8,128)(2,1)S(1)} %slice.78), channel_id=1, source_target_pairs={{0,8},{1,9},{2,10},{3,11},{4,12},{5,13},{6,14},{7,15},{8,0},{9,1},... | collective-permute-start | bytes 491528 | tf_op jit(solution)/shard_map/ppermute | solution.py:30
  84.7 17.8 %collective-permute-done.14 = bf16[4,320,512]{2,1,0:T(8,128)(2,1)S(1)} collective-permute-done((bf16[4,320,512]{2,1,0:T(8,128)(2,1)}, bf16[4,320,512]{2,1,0:T(8,128)(2,1)S(1)}, u32[]{:S(2)}, u32[]{:S(2)}) %collective-permute-start.14) | collective-permute-done | bytes 1310752 | tf_op jit(solution)/shard_map/ppermute | solution.py:30
  102.5 2.2 %fusion = f32[256,1024]{1,0:T(8,128)S(1)} fusion(bf16[1280,512]{1,0:T(8,128)(2,1)S(1)} %bitcast.116, bf16[1280,512]{1,0:T(8,128)(2,1)} %bitcast.18, bf16[1280,128]{1,0:T(8,128)(2,1)S(1)} %collective-permute-done.12, bf16[1280,128]{1,0:T(8,128)(2,1)S(1)} %bitcast.105), kind=kOutput, calls=%fused_computation.1 | convolution fusion | flops 677642240 | bytes 4325376 | tf_op jit(solution)/shard_map/dot_general | solution.py:267
  104.9 1.1 collective-permute-done.13
  105.9 2.2 %fusion.1 = f32[256,1024]{1,0:T(8,128)S(1)} fusion(bf16[1280,512]{1,0:T(8,128)(2,1)S(1)} %bitcast.117, bf16[1280,512]{1,0:T(8,128)(2,1)} %bitcast.18, bf16[640,128]{1,0:T(8,128)(2,1)S(1)} %collective-permute-done.13, bf16[640,128]{1,0:T(8,128)(2,1)S(1)} %collective-permute-done.11, bf16[1280,128]{1,0:T(8,128)(2,1)S(1)} %collective-permute-done.10), kind=kOutput, calls=%fused_computation.2 | convolution fusion | flops 678297600 | bytes 4325376 | tf_op jit(solution)/shard_map/dot_general | solution.py:267
  108.1 0.1 bitcast_add_fusion
  108.2 1.5 %collective-permute-start.17 = (bf16[64,1024]{1,0:T(8,128)(2,1)S(1)}, bf16[64,1024]{1,0:T(8,128)(2,1)S(1)}, u32[]{:S(2)}, u32[]{:S(2)}) collective-permute-start(bf16[64,1024]{1,0:T(8,128)(2,1)S(1)} %fusion.34), channel_id=1, source_target_pairs={{0,2},{1,3},{2,0},{3,1},{4,6},{5,7},{6,4},{7,5},{8,10},{9,11},{10,... | collective-permute-start | bytes 393224 | tf_op jit(solution)/shard_map/ppermute | solution.py:30
  109.9 3.8 %collective-permute-done.17 = bf16[64,1024]{1,0:T(8,128)(2,1)S(1)} collective-permute-done((bf16[64,1024]{1,0:T(8,128)(2,1)S(1)}, bf16[64,1024]{1,0:T(8,128)(2,1)S(1)}, u32[]{:S(2)}, u32[]{:S(2)}) %collective-permute-start.17) | collective-permute-done | bytes 131104 | tf_op jit(solution)/shard_map/ppermute | solution.py:30
  113.8 0.1 bitcast_add_fusion.1
  113.9 1.5 %collective-permute-start.19 = (bf16[64,1024]{1,0:T(8,128)(2,1)S(1)}, bf16[64,1024]{1,0:T(8,128)(2,1)S(1)}, u32[]{:S(2)}, u32[]{:S(2)}) collective-permute-start(bf16[64,1024]{1,0:T(8,128)(2,1)S(1)} %fusion.33), channel_id=1, source_target_pairs={{0,2},{1,3},{2,0},{3,1},{4,6},{5,7},{6,4},{7,5},{8,10},{9,11},{10,... | collective-permute-start | bytes 393224 | tf_op jit(solution)/shard_map/ppermute | solution.py:30
  115.5 1.5 %collective-permute-start.18 = (bf16[64,1024]{1,0:T(8,128)(2,1)S(1)}, bf16[64,1024]{1,0:T(8,128)(2,1)S(1)}, u32[]{:S(2)}, u32[]{:S(2)}) collective-permute-start(bf16[64,1024]{1,0:T(8,128)(2,1)S(1)} %fusion.32.p0), channel_id=1, source_target_pairs={{0,6},{1,7},{2,4},{3,5},{4,2},{5,3},{6,0},{7,1},{8,14},{9,15},{10,... | collective-permute-start | bytes 393224 | tf_op jit(solution)/shard_map/ppermute | solution.py:30
  116.9 3.1 %collective-permute-done.19 = bf16[64,1024]{1,0:T(8,128)(2,1)S(1)} collective-permute-done((bf16[64,1024]{1,0:T(8,128)(2,1)S(1)}, bf16[64,1024]{1,0:T(8,128)(2,1)S(1)}, u32[]{:S(2)}, u32[]{:S(2)}) %collective-permute-start.19) | collective-permute-done | bytes 131104 | tf_op jit(solution)/shard_map/ppermute | solution.py:30
  120.2 3.8 %collective-permute-start.21 = (bf16[64,1024]{1,0:T(8,128)(2,1)S(1)}, bf16[64,1024]{1,0:T(8,128)(2,1)S(1)}, u32[]{:S(2)}, u32[]{:S(2)}) collective-permute-start(bf16[64,1024]{1,0:T(8,128)(2,1)S(1)} %fusion.30), channel_id=1, source_target_pairs={{0,14},{1,15},{2,12},{3,13},{4,10},{5,11},{6,8},{7,9},{8,6},{9,7},... | collective-permute-start | bytes 393224 | tf_op jit(solution)/shard_map/ppermute | solution.py:30
  124.0 0.6 dynamic_slice.26
  125.2 0.1 pad_add_fusion.scalars
  125.3 3.0 %collective-permute-done.21.p3 = bf16[64,1024]{1,0:T(8,128)(2,1)S(1)} collective-permute-done((bf16[64,1024]{1,0:T(8,128)(2,1)S(1)}, bf16[64,1024]{1,0:T(8,128)(2,1)S(1)}, u32[]{:S(2)}, u32[]{:S(2)}) %collective-permute-start.21) | collective-permute-done | bytes 131104 | tf_op jit(solution)/shard_map/ppermute | solution.py:30
  128.3 1.4 %shard_map.120 = bf16[64,4096]{1,0:T(8,128)(2,1)} custom-call(s32[2]{0:T(128)S(1)} %pad_add_fusion.scalars, bf16[64,1024]{1,0:T(8,128)(2,1)S(1)} %fusion.32.p0, bf16[64,1024]{1,0:T(8,128)(2,1)S(1)} %collective-permute-done.18.p1, bf16[64,1024]{1,0:T(8,128)(2,1)S(1)} %collective-permute-done.20.p2, bf16[64,1024]{1,0:T(8,128)(2,1)S(1)} %collective-permute-done.21.p3), custom_call_target="tpu_custom_call" | custom-call | tf_op jit(solution)/shard_map/pallas_call | solution.py:170
  (59 shorter events, 0.8 us)
Async XLA Ops:
  0.0 47.1 %copy-start = (bf16[1280,320]{0,1:T(8,128)(2,1)S(1)}, bf16[1280,320]{0,1:T(8,128)(2,1)}, u32[]{:S(2)}) copy-start(bf16[1280,320]{0,1:T(8,128)(2,1)} %param.18) | copy-start | bytes 2457604
  0.0 5.0 %copy-start.9 = (s32[16]{0:T(128)S(1)}, s32[16]{0:T(128)}, u32[]{:S(2)}) copy-start(s32[16]{0:T(128)} %param.13) | copy-start | bytes 196
  2.0 11.0 %collective-permute-start = (bf16[320,512]{1,0:T(8,128)(2,1)}, bf16[320,512]{1,0:T(8,128)(2,1)}, u32[]{:S(2)}, u32[]{:S(2)}) collective-permute-start(bf16[320,512]{1,0:T(8,128)(2,1)} %get-tuple-element.15), channel_id=1, source_target_pairs={{0,4},{1,5},{2,6},{3,7},{4,0},{5,1},{6,2},{7,3},{8,12},{9,13},{10,... | collective-permute-start | bytes 983048 | tf_op jit(solution)/shard_map/ppermute | solution.py:30
  5.8 1.7 %copy-start.1 = (bf16[1280,3,320]{0,2,1:T(8,128)(2,1)S(1)}, bf16[1280,3,320]{0,2,1:T(8,128)(2,1)}, u32[]{:S(2)}) copy-start(bf16[1280,3,320]{0,2,1:T(8,128)(2,1)} %param.16) | copy-start | bytes 7372804
  7.5 0.7 copy-start.6
  7.5 0.8 copy-start.4
  7.5 0.8 copy-start.5
  14.1 18.0 %copy-start.2 = (bf16[320,512]{1,0:T(8,128)(2,1)}, bf16[320,512]{1,0:T(8,128)(2,1)S(1)}, u32[]{:S(2)}) copy-start(bf16[320,512]{1,0:T(8,128)(2,1)S(1)} %broadcast_select_fusion.8.own) | copy-start | bytes 983044
  14.1 8.9 %collective-permute-start.2 = (bf16[320,512]{1,0:T(8,128)(2,1)S(1)}, bf16[320,512]{1,0:T(8,128)(2,1)S(1)}, u32[]{:S(2)}, u32[]{:S(2)}) collective-permute-start(bf16[320,512]{1,0:T(8,128)(2,1)S(1)} %broadcast_select_fusion.8.own), channel_id=1, source_target_pairs={{0,2},{1,3},{2,0},{3,1},{4,6},{5,7},{6,4},{7,5},{8,10},{9,11},{10,... | collective-permute-start | bytes 983048 | tf_op jit(solution)/shard_map/ppermute | solution.py:30
  15.9 7.4 %collective-permute-start.1 = (bf16[320,512]{1,0:T(8,128)(2,1)S(1)}, bf16[320,512]{1,0:T(8,128)(2,1)S(1)}, u32[]{:S(2)}, u32[]{:S(2)}) collective-permute-start(bf16[320,512]{1,0:T(8,128)(2,1)S(1)} %broadcast_select_fusion.8.own), channel_id=1, source_target_pairs={{0,1},{1,0},{2,3},{3,2},{4,5},{5,4},{6,7},{7,6},{8,9},{9,8},{10,11... | collective-permute-start | bytes 983048 | tf_op jit(solution)/shard_map/ppermute | solution.py:30
  23.0 1.6 %collective-permute-start.3 = (bf16[320,512]{1,0:T(8,128)(2,1)S(1)}, bf16[320,512]{1,0:T(8,128)(2,1)S(1)}, u32[]{:S(2)}, u32[]{:S(2)}) collective-permute-start(bf16[320,512]{1,0:T(8,128)(2,1)S(1)} %collective-permute-done.2.far), channel_id=1, source_target_pairs={{0,1},{1,0},{2,3},{3,2},{4,5},{5,4},{6,7},{7,6},{8,9},{9,8},{10,11... | collective-permute-start | bytes 983048 | tf_op jit(solution)/shard_map/ppermute | solution.py:30
  23.3 21.3 %copy-start.10 = (f32[320]{0:T(512)S(1)}, f32[320]{0:T(512)}, u32[]{:S(2)}) copy-start(f32[320]{0:T(512)} %param.19) | copy-start | bytes 3844
  32.1 10.0 %collective-permute-start.4 = (bf16[320,512]{1,0:T(8,128)(2,1)}, bf16[320,512]{1,0:T(8,128)(2,1)S(1)}, u32[]{:S(2)}, u32[]{:S(2)}) collective-permute-start(bf16[320,512]{1,0:T(8,128)(2,1)} %shard_map.119), channel_id=1, source_target_pairs={{0,2},{1,3},{2,0},{3,1},{4,6},{5,7},{6,4},{7,5},{8,10},{9,11},{10,... | collective-permute-start | bytes 983048 | tf_op jit(solution)/shard_map/ppermute | solution.py:30
  33.5 12.5 %collective-permute-start.6 = (bf16[320,512]{1,0:T(8,128)(2,1)}, bf16[320,512]{1,0:T(8,128)(2,1)S(1)}, u32[]{:S(2)}, u32[]{:S(2)}) collective-permute-start(bf16[320,512]{1,0:T(8,128)(2,1)} %shard_map.119), channel_id=1, source_target_pairs={{0,1},{1,0},{2,3},{3,2},{4,5},{5,4},{6,7},{7,6},{8,9},{9,8},{10,11... | collective-permute-start | bytes 983048 | tf_op jit(solution)/shard_map/ppermute | solution.py:30
  42.0 4.0 %collective-permute-start.5 = (bf16[320,512]{1,0:T(8,128)(2,1)S(1)}, bf16[320,512]{1,0:T(8,128)(2,1)S(1)}, u32[]{:S(2)}, u32[]{:S(2)}) collective-permute-start(bf16[320,512]{1,0:T(8,128)(2,1)S(1)} %collective-permute-done.4), channel_id=1, source_target_pairs={{0,1},{1,0},{2,3},{3,2},{4,5},{5,4},{6,7},{7,6},{8,9},{9,8},{10,11... | collective-permute-start | bytes 983048 | tf_op jit(solution)/shard_map/ppermute | solution.py:30
  42.0 60.5 %collective-permute-start.14 = (bf16[4,320,512]{2,1,0:T(8,128)(2,1)}, bf16[4,320,512]{2,1,0:T(8,128)(2,1)S(1)}, u32[]{:S(2)}, u32[]{:S(2)}) collective-permute-start(bf16[4,320,512]{2,1,0:T(8,128)(2,1)} %param.22), channel_id=1, source_target_pairs={{0,16},{1,17},{2,18},{3,19},{4,20},{5,21},{6,22},{7,23},{8,24},{9,... | collective-permute-start | bytes 3932168 | tf_op jit(solution)/shard_map/ppermute | solution.py:30
  47.1 5.5 %copy-start.7 = (f32[320]{0:T(512)S(1)}, f32[320]{0:T(512)}, u32[]{:S(2)}) copy-start(f32[320]{0:T(512)} %param.21) | copy-start | bytes 3844
  47.1 5.5 %copy-start.8 = (f32[320]{0:T(512)S(1)}, f32[320]{0:T(512)}, u32[]{:S(2)}) copy-start(f32[320]{0:T(512)} %param.20) | copy-start | bytes 3844
  47.2 8.9 %copy-start.3 = (f32[4096]{0:T(1024)S(1)}, f32[4096]{0:T(1024)}, u32[]{:S(2)}) copy-start(f32[4096]{0:T(1024)} %param.23) | copy-start | bytes 49156
  47.8 1.9 %collective-permute-start.7 = (f32[2,512]{1,0:T(2,128)S(1)}, f32[2,512]{1,0:T(2,128)S(1)}, u32[]{:S(2)}, u32[]{:S(2)}) collective-permute-start(f32[2,512]{1,0:T(2,128)S(1)} %pad_maximum_fusion.3), channel_id=1, source_target_pairs={{0,1},{1,0},{2,3},{3,2},{4,5},{5,4},{6,7},{7,6},{8,9},{9,8},{10,11... | collective-permute-start | bytes 12296 | tf_op jit(solution)/shard_map/ppermute | solution.py:30
  48.1 3.6 %collective-permute-start.8 = (f32[2,512]{1,0:T(2,128)S(1)}, f32[2,512]{1,0:T(2,128)S(1)}, u32[]{:S(2)}, u32[]{:S(2)}) collective-permute-start(f32[2,512]{1,0:T(2,128)S(1)} %pad_maximum_fusion.3), channel_id=1, source_target_pairs={{0,2},{1,3},{2,0},{3,1},{4,6},{5,7},{6,4},{7,5},{8,10},{9,11},{10,... | collective-permute-start | bytes 12296 | tf_op jit(solution)/shard_map/ppermute | solution.py:30
  49.6 3.0 %collective-permute-start.9 = (f32[2,512]{1,0:T(2,128)S(1)}, f32[2,512]{1,0:T(2,128)S(1)}, u32[]{:S(2)}, u32[]{:S(2)}) collective-permute-start(f32[2,512]{1,0:T(2,128)S(1)} %pad_maximum_fusion.3), channel_id=1, source_target_pairs={{0,3},{1,2},{2,1},{3,0},{4,7},{5,6},{6,5},{7,4},{8,11},{9,10},{10,... | collective-permute-start | bytes 12296 | tf_op jit(solution)/shard_map/ppermute | solution.py:30
  52.8 27.7 %collective-permute-start.10 = (bf16[1280,128]{1,0:T(8,128)(2,1)S(1)}, bf16[1280,128]{1,0:T(8,128)(2,1)S(1)}, u32[]{:S(2)}, u32[]{:S(2)}) collective-permute-start(bf16[1280,128]{1,0:T(8,128)(2,1)S(1)} %bitcast.103), channel_id=1, source_target_pairs={{0,8},{1,9},{2,10},{3,11},{4,12},{5,13},{6,14},{7,15},{8,0},{9,1},... | collective-permute-start | bytes 983048 | tf_op jit(solution)/shard_map/ppermute | solution.py:30
  54.5 27.7 %collective-permute-start.12 = (bf16[1280,128]{1,0:T(8,128)(2,1)S(1)}, bf16[1280,128]{1,0:T(8,128)(2,1)S(1)}, u32[]{:S(2)}, u32[]{:S(2)}) collective-permute-start(bf16[1280,128]{1,0:T(8,128)(2,1)S(1)} %bitcast.104), channel_id=1, source_target_pairs={{0,4},{1,5},{2,6},{3,7},{4,0},{5,1},{6,2},{7,3},{8,12},{9,13},{10,... | collective-permute-start | bytes 983048 | tf_op jit(solution)/shard_map/ppermute | solution.py:30
  80.6 24.3 %collective-permute-start.11 = (bf16[640,128]{1,0:T(8,128)(2,1)S(1)}, bf16[640,128]{1,0:T(8,128)(2,1)S(1)}, u32[]{:S(2)}, u32[]{:S(2)}) collective-permute-start(bf16[640,128]{1,0:T(8,128)(2,1)S(1)} %slice.77), channel_id=1, source_target_pairs={{0,4},{1,5},{2,6},{3,7},{4,0},{5,1},{6,2},{7,3},{8,12},{9,13},{10,... | collective-permute-start | bytes 491528 | tf_op jit(solution)/shard_map/ppermute | solution.py:30
  82.2 23.8 %collective-permute-start.13 = (bf16[640,128]{1,0:T(8,128)(2,1)S(1)}, bf16[640,128]{1,0:T(8,128)(2,1)S(1)}, u32[]{:S(2)}, u32[]{:S(2)}) collective-permute-start(bf16[640,128]{1,0:T(8,128)(2,1)S(1)} %slice.78), channel_id=1, source_target_pairs={{0,8},{1,9},{2,10},{3,11},{4,12},{5,13},{6,14},{7,15},{8,0},{9,1},... | collective-permute-start | bytes 491528 | tf_op jit(solution)/shard_map/ppermute | solution.py:30
  104.8 3.4 %collective-permute-start.16 = (bf16[2,64,1024]{2,1,0:T(8,128)(2,1)S(1)}, bf16[2,64,1024]{2,1,0:T(8,128)(2,1)S(1)}, u32[]{:S(2)}, u32[]{:S(2)}) collective-permute-start(bf16[2,64,1024]{2,1,0:T(8,128)(2,1)S(1)} %fusion.28), channel_id=1, source_target_pairs={{0,1},{1,0},{2,3},{3,2},{4,5},{5,4},{6,7},{7,6},{8,9},{9,8},{10,11... | collective-permute-start | bytes 786440 | tf_op jit(solution)/shard_map/ppermute | solution.py:30
  108.2 5.5 %collective-permute-start.17 = (bf16[64,1024]{1,0:T(8,128)(2,1)S(1)}, bf16[64,1024]{1,0:T(8,128)(2,1)S(1)}, u32[]{:S(2)}, u32[]{:S(2)}) collective-permute-start(bf16[64,1024]{1,0:T(8,128)(2,1)S(1)} %fusion.34), channel_id=1, source_target_pairs={{0,2},{1,3},{2,0},{3,1},{4,6},{5,7},{6,4},{7,5},{8,10},{9,11},{10,... | collective-permute-start | bytes 393224 | tf_op jit(solution)/shard_map/ppermute | solution.py:30
  109.8 4.0 %collective-permute-start.15 = (bf16[2,64,1024]{2,1,0:T(8,128)(2,1)S(1)}, bf16[2,64,1024]{2,1,0:T(8,128)(2,1)S(1)}, u32[]{:S(2)}, u32[]{:S(2)}) collective-permute-start(bf16[2,64,1024]{2,1,0:T(8,128)(2,1)S(1)} %fusion.27), channel_id=1, source_target_pairs={{0,1},{1,0},{2,3},{3,2},{4,5},{5,4},{6,7},{7,6},{8,9},{9,8},{10,11... | collective-permute-start | bytes 786440 | tf_op jit(solution)/shard_map/ppermute | solution.py:30
  113.9 6.1 %collective-permute-start.19 = (bf16[64,1024]{1,0:T(8,128)(2,1)S(1)}, bf16[64,1024]{1,0:T(8,128)(2,1)S(1)}, u32[]{:S(2)}, u32[]{:S(2)}) collective-permute-start(bf16[64,1024]{1,0:T(8,128)(2,1)S(1)} %fusion.33), channel_id=1, source_target_pairs={{0,2},{1,3},{2,0},{3,1},{4,6},{5,7},{6,4},{7,5},{8,10},{9,11},{10,... | collective-permute-start | bytes 393224 | tf_op jit(solution)/shard_map/ppermute | solution.py:30
  115.5 9.8 %collective-permute-start.18 = (bf16[64,1024]{1,0:T(8,128)(2,1)S(1)}, bf16[64,1024]{1,0:T(8,128)(2,1)S(1)}, u32[]{:S(2)}, u32[]{:S(2)}) collective-permute-start(bf16[64,1024]{1,0:T(8,128)(2,1)S(1)} %fusion.32.p0), channel_id=1, source_target_pairs={{0,6},{1,7},{2,4},{3,5},{4,2},{5,3},{6,0},{7,1},{8,14},{9,15},{10,... | collective-permute-start | bytes 393224 | tf_op jit(solution)/shard_map/ppermute | solution.py:30
  120.1 5.2 %collective-permute-start.20 = (bf16[64,1024]{1,0:T(8,128)(2,1)S(1)}, bf16[64,1024]{1,0:T(8,128)(2,1)S(1)}, u32[]{:S(2)}, u32[]{:S(2)}) collective-permute-start(bf16[64,1024]{1,0:T(8,128)(2,1)S(1)} %fusion.30), channel_id=1, source_target_pairs={{0,8},{1,9},{2,10},{3,11},{4,12},{5,13},{6,14},{7,15},{8,0},{9,1},... | collective-permute-start | bytes 393224 | tf_op jit(solution)/shard_map/ppermute | solution.py:30
  120.2 8.1 %collective-permute-start.21 = (bf16[64,1024]{1,0:T(8,128)(2,1)S(1)}, bf16[64,1024]{1,0:T(8,128)(2,1)S(1)}, u32[]{:S(2)}, u32[]{:S(2)}) collective-permute-start(bf16[64,1024]{1,0:T(8,128)(2,1)S(1)} %fusion.30), channel_id=1, source_target_pairs={{0,14},{1,15},{2,12},{3,13},{4,10},{5,11},{6,8},{7,9},{8,6},{9,7},... | collective-permute-start | bytes 393224 | tf_op jit(solution)/shard_map/ppermute | solution.py:30

commit v2 on v1

--- a/solution.py
+++ b/solution.py
@@ -149,6 +149,33 @@
     )(x)
 
 
+def join_kernel(*refs):
+    sources, out, sems = refs[:-2], refs[-2], refs[-1]
+    width = out.shape[1] // len(sources)
+    copies = [
+        pltpu.make_async_copy(source, out.at[:, i * width : (i + 1) * width], sems.at[i])
+        for i, source in enumerate(sources)
+    ]
+    for copy in copies:
+        copy.start()
+    for copy in copies:
+        copy.wait()
+
+
+def joined(columns):
+    rows, width = columns[0].shape
+    if width % LANES > 0:
+        return jnp.concatenate(columns, axis=1)
+    return pl.pallas_call(
+        join_kernel,
+        out_shape=pltpu.VMEM((rows, width * len(columns)), columns[0].dtype),
+        in_specs=[pl.BlockSpec(memory_space=pl.ANY)] * len(columns),
+        out_specs=VMEM,
+        scratch_shapes=[pltpu.SemaphoreType.DMA((len(columns),))],
+        compiler_params=pltpu.CompilerParams(vmem_limit_bytes=8 << 20),
+    )(*columns)
+
+
 def place_kernel(block_width, scalars, p0, p1, p2, p3, out):
     rank = scalars[0]
     rows, total = p0.shape
@@ -219,7 +246,7 @@
     while bit < ranks:
         columns = columns + [swap(c, bit) for c in columns]
         bit *= 2
-    held = jnp.concatenate([c.reshape(MERGE * width, block_width) for c in columns], axis=1)
+    held = joined([c.reshape(MERGE * width, block_width) for c in columns])
 
     source = jnp.arange(TILE, dtype=jnp.int32)
     order = (source % MERGE * rows + source // MERGE)[:, None] == source[None, :]
@@ -250,7 +277,7 @@
 
     one = swap(merged, 1)
     two = swap(merged, 2)
-    cut = MERGE * width // 2
+    cut = MERGE * width * 3 // 8
     three = swap(two[:cut], 1)
     three = jnp.concatenate([three, swap(one[cut:], 2)], axis=0)
 
@@ -262,24 +289,28 @@
 
     low = jnp.bitwise_and(me, 1) == 1
 
-    def reduced(first, second, before=None):
-        lines = jnp.concatenate([first, second], axis=1)
+    def core_sum(lines):
         product = lax.dot_general(
             lines, held, (((0,), (0,)), ((), ())), preferred_element_type=jnp.float32
-        ).reshape(2, 2, rows // 2, held.shape[1])
+        ).reshape(-1, 2, rows // 2, held.shape[1])
         sent = jnp.where(low, product[:, 0], product[:, 1]).astype(jnp.bfloat16)
         kept = jnp.where(low, product[:, 1], product[:, 0])
-        half = kept + swap(sent, 0, 1).astype(jnp.float32)
-        kept = jnp.where(high, half[1], half[0])
-        sent = jnp.where(high, half[0], half[1]).astype(jnp.bfloat16)
+        return kept + swap(sent, 0, 1).astype(jnp.float32)
+
+    def reduced(first, second, before=None):
+        kept = jnp.where(high, second, first)
+        sent = jnp.where(high, first, second).astype(jnp.bfloat16)
         if before is not None:
             sent, before = lax.optimization_barrier((sent, before))
         other = swap(sent, 0, 2)
         total = kept + other.astype(jnp.float32)
         return (total + bias).astype(jnp.bfloat16), before
 
-    near, _ = reduced(merged, one)
-    pair, near = reduced(two, three, near)
+    half = core_sum(jnp.concatenate([merged, one], axis=1))
+    near, _ = reduced(half[0], half[1])
+    first = core_sum(two)[0]
+    last = core_sum(three)[0]
+    pair, near = reduced(first, last, near)
     pieces = [near, swap(near, 1, 2)]
     pieces += [swap(pair, 2, 0), swap(pair, 3, 2)]
 

time: 130 us -> 143 us (1.10)
  waiting for transfers between devices: 77.2 us -> 92.1 us
  matrix products: 6.37 us -> 3.95 us
    ppermute x22 -> x23, waiting for transfers between devices: 77.2 us -> 92.1 us  [swap(): lax.ppermute(x, ('dp', 'tensor'), [(i, i ^ flip) for i in range(total)])]
    dot_general x2 -> x3, matrix products: 4.35 us -> 1.92 us  [core_sum(): lax.dot_general(lines, held, (((0,), (0,)), ((), ())), preferred_element_...]
    ppermute x22 -> x23, starting transfers between devices: 26.5 us -> 25.3 us  [swap(): lax.ppermute(x, ('dp', 'tensor'), [(i, i ^ flip) for i in range(total)])]
  transfers between devices with their start and end apart: 22 -> 23, of which waited for: 12 -> 12; matrix products, arithmetic and copies ran while one was open for 7% -> 6% of each run, Pallas kernels for 0% -> 1%
where the time goes in v2:
time: 143 us; the launch traced here: 142 us
  waiting for transfers between devices  92.1 us (64%)
  starting transfers between devices  25.3 us (18%)
  Pallas kernels  10.4 us (7%)
  local copies, waits for them, and re-layouts  5.89 us (4%)
  matrix products  3.95 us (3%)
  other arithmetic  3.11 us (2%)
  between operations  1.67 us (1%)
    ppermute x23, waiting for transfers between devices, swap(): lax.ppermute(x, ('dp', 'tensor'), [(i, i ^ flip) for i in range(total)])  92.1 us
    ppermute x23, starting transfers between devices, swap(): lax.ppermute(x, ('dp', 'tensor'), [(i, i ^ flip) for i in range(total)])  25.3 us
    pallas_call x1, Pallas kernels, attend(): pl.pallas_call(attend_kernel, out_shape=pltpu.VMEM((width, rows), jnp.bfl...  7.42 us
  transfers between devices with their start and end apart: 23, of which 12 were waited for; matrix products, arithmetic and copies ran while one was open for 6% of the time, Pallas kernels for 1%

profile of v2, /device:TPU:0, one launch (start us, length us, event | category | flops | bytes accessed | tf_op | source)
XLA Modules:
  0.0 142.5 jit_solution(1238074911670764977)
XLA Ops:
  0.0 2.0 %fusion.48 = (bf16[320,512]{1,0:T(8,128)(2,1)}, bf16[320,512]{1,0:T(8,128)(2,1)}) fusion(bf16[320,1024]{1,0:T(8,128)(2,1)} %bitcast.108), kind=kLoop, calls=%fused_computation.87 | loop fusion | bytes 1310720 | tf_op jit(solution)/shard_map/slice | solution.py:240
  2.0 3.1 %collective-permute-start = (bf16[320,512]{1,0:T(8,128)(2,1)}, bf16[320,512]{1,0:T(8,128)(2,1)}, u32[]{:S(2)}, u32[]{:S(2)}) collective-permute-start(bf16[320,512]{1,0:T(8,128)(2,1)} %get-tuple-element.15), channel_id=1, source_target_pairs={{0,4},{1,5},{2,6},{3,7},{4,0},{5,1},{6,2},{7,3},{8,12},{9,13},{10,... | collective-permute-start | bytes 983048 | tf_op jit(solution)/shard_map/ppermute | solution.py:30
  5.1 0.8 fusion.49
  5.9 0.6 slice.58
  6.5 1.7 %copy-done.1 = bf16[1280,3,320]{0,2,1:T(8,128)(2,1)S(1)} copy-done((bf16[1280,3,320]{0,2,1:T(8,128)(2,1)S(1)}, bf16[1280,3,320]{0,2,1:T(8,128)(2,1)}, u32[]{:S(2)}) %copy-start.1) | copy-done | bytes 2457624
  8.2 0.3 shard_map.118.weight
  9.3 3.9 %collective-permute-done = bf16[320,512]{1,0:T(8,128)(2,1)} collective-permute-done((bf16[320,512]{1,0:T(8,128)(2,1)}, bf16[320,512]{1,0:T(8,128)(2,1)}, u32[]{:S(2)}, u32[]{:S(2)}) %collective-permute-start) | collective-permute-done | bytes 327712 | tf_op jit(solution)/shard_map/ppermute | solution.py:30
  13.1 1.0 broadcast_select_fusion.8.own
  14.2 1.8 %collective-permute-start.2 = (bf16[320,512]{1,0:T(8,128)(2,1)S(1)}, bf16[320,512]{1,0:T(8,128)(2,1)S(1)}, u32[]{:S(2)}, u32[]{:S(2)}) collective-permute-start(bf16[320,512]{1,0:T(8,128)(2,1)S(1)} %broadcast_select_fusion.8.own), channel_id=1, source_target_pairs={{0,2},{1,3},{2,0},{3,1},{4,6},{5,7},{6,4},{7,5},{8,10},{9,11},{10,... | collective-permute-start | bytes 983048 | tf_op jit(solution)/shard_map/ppermute | solution.py:30
  16.0 7.1 %collective-permute-done.2.far = bf16[320,512]{1,0:T(8,128)(2,1)S(1)} collective-permute-done((bf16[320,512]{1,0:T(8,128)(2,1)S(1)}, bf16[320,512]{1,0:T(8,128)(2,1)S(1)}, u32[]{:S(2)}, u32[]{:S(2)}) %collective-permute-start.2) | collective-permute-done | bytes 327712 | tf_op jit(solution)/shard_map/ppermute | solution.py:30
  23.2 0.2 fusion.14.order
  23.3 1.4 collective-permute-done.3.cross
  24.7 7.4 %shard_map.119 = bf16[320,512]{1,0:T(8,128)(2,1)} custom-call(s32[2]{0:T(128)S(1)} %pad_add_fusion.1.scalars, bf16[320,512]{1,0:T(8,128)(2,1)S(1)} %broadcast_select_fusion.8.own, bf16[320,512]{1,0:T(8,128)(2,1)S(1)} %collective-permute-done.1.near, bf16[320,512]{1,0:T(8,128)(2,1)S(1)} %collective-permute-done.2.far, ...), custom_call_target="tpu_custom_call" | custom-call | tf_op jit(solution)/shard_map/pallas_call | solution.py:124
  32.1 1.4 %collective-permute-start.4 = (bf16[320,512]{1,0:T(8,128)(2,1)}, bf16[320,512]{1,0:T(8,128)(2,1)S(1)}, u32[]{:S(2)}, u32[]{:S(2)}) collective-permute-start(bf16[320,512]{1,0:T(8,128)(2,1)} %shard_map.119), channel_id=1, source_target_pairs={{0,2},{1,3},{2,0},{3,1},{4,6},{5,7},{6,4},{7,5},{8,10},{9,11},{10,... | collective-permute-start | bytes 983048 | tf_op jit(solution)/shard_map/ppermute | solution.py:30
  33.6 8.5 %collective-permute-done.4 = bf16[320,512]{1,0:T(8,128)(2,1)S(1)} collective-permute-done((bf16[320,512]{1,0:T(8,128)(2,1)}, bf16[320,512]{1,0:T(8,128)(2,1)S(1)}, u32[]{:S(2)}, u32[]{:S(2)}) %collective-permute-start.4) | collective-permute-done | bytes 327712 | tf_op jit(solution)/shard_map/ppermute | solution.py:30
  42.1 2.5 %collective-permute-start.11 = (bf16[4,320,512]{2,1,0:T(8,128)(2,1)}, bf16[4,320,512]{2,1,0:T(8,128)(2,1)S(1)}, u32[]{:S(2)}, u32[]{:S(2)}) collective-permute-start(bf16[4,320,512]{2,1,0:T(8,128)(2,1)} %param.22), channel_id=1, source_target_pairs={{0,16},{1,17},{2,18},{3,19},{4,20},{5,21},{6,22},{7,23},{8,24},{9,... | collective-permute-start | bytes 3932168 | tf_op jit(solution)/shard_map/ppermute | solution.py:30
  44.6 1.4 convolution_add_fusion
  46.1 1.1 broadcast_select_fusion.7
  47.2 0.6 fusion.47
  47.9 0.3 collective-permute-start.7
  48.2 1.5 %collective-permute-start.8 = (f32[2,512]{1,0:T(2,128)S(1)}, f32[2,512]{1,0:T(2,128)S(1)}, u32[]{:S(2)}, u32[]{:S(2)}) collective-permute-start(f32[2,512]{1,0:T(2,128)S(1)} %pad_maximum_fusion), channel_id=1, source_target_pairs={{0,2},{1,3},{2,0},{3,1},{4,6},{5,7},{6,4},{7,5},{8,10},{9,11},{10,... | collective-permute-start | bytes 12296 | tf_op jit(solution)/shard_map/ppermute | solution.py:30
  49.6 0.1 collective-permute-start.9
  49.8 2.0 %collective-permute-done.8 = f32[2,512]{1,0:T(2,128)S(1)} collective-permute-done((f32[2,512]{1,0:T(2,128)S(1)}, f32[2,512]{1,0:T(2,128)S(1)}, u32[]{:S(2)}, u32[]{:S(2)}) %collective-permute-start.8) | collective-permute-done | bytes 4128 | tf_op jit(solution)/shard_map/ppermute | solution.py:30
  51.8 0.9 collective-permute-done.9
  52.7 0.2 copy_bitcast_fusion
  52.9 1.6 %collective-permute-start.14 = (bf16[1280,128]{1,0:T(8,128)(2,1)S(1)}, bf16[1280,128]{1,0:T(8,128)(2,1)S(1)}, u32[]{:S(2)}, u32[]{:S(2)}) collective-permute-start(bf16[1280,128]{1,0:T(8,128)(2,1)S(1)} %bitcast.109), channel_id=1, source_target_pairs={{0,4},{1,5},{2,6},{3,7},{4,0},{5,1},{6,2},{7,3},{8,12},{9,13},{10,... | collective-permute-start | bytes 983048 | tf_op jit(solution)/shard_map/ppermute | solution.py:30
  54.6 47.9 %collective-permute-done.11 = bf16[4,320,512]{2,1,0:T(8,128)(2,1)S(1)} collective-permute-done((bf16[4,320,512]{2,1,0:T(8,128)(2,1)}, bf16[4,320,512]{2,1,0:T(8,128)(2,1)S(1)}, u32[]{:S(2)}, u32[]{:S(2)}) %collective-permute-start.11) | collective-permute-done | bytes 1310752 | tf_op jit(solution)/shard_map/ppermute | solution.py:30
  102.5 1.3 shard_map.120
  103.8 0.8 collective-permute-start.10
  104.6 0.9 fusion.15
  105.6 1.4 collective-permute-start.15
  107.0 7.5 %collective-permute-done.10 = bf16[1280,128]{1,0:T(8,128)(2,1)S(1)} collective-permute-done((bf16[1280,128]{1,0:T(8,128)(2,1)S(1)}, bf16[1280,128]{1,0:T(8,128)(2,1)S(1)}, u32[]{:S(2)}, u32[]{:S(2)}) %collective-permute-start.10) | collective-permute-done | bytes 327712 | tf_op jit(solution)/shard_map/ppermute | solution.py:30
  114.5 1.5 %collective-permute-start.13 = (bf16[480,128]{1,0:T(8,128)(2,1)S(1)}, bf16[480,128]{1,0:T(8,128)(2,1)S(1)}, u32[]{:S(2)}, u32[]{:S(2)}) collective-permute-start(bf16[480,128]{1,0:T(8,128)(2,1)S(1)} %slice.77), channel_id=1, source_target_pairs={{0,4},{1,5},{2,6},{3,7},{4,0},{5,1},{6,2},{7,3},{8,12},{9,13},{10,... | collective-permute-start | bytes 368648 | tf_op jit(solution)/shard_map/ppermute | solution.py:30
  116.0 0.5 fusion.50
  116.7 2.8 %collective-permute-done.13 = bf16[480,128]{1,0:T(8,128)(2,1)S(1)} collective-permute-done((bf16[480,128]{1,0:T(8,128)(2,1)S(1)}, bf16[480,128]{1,0:T(8,128)(2,1)S(1)}, u32[]{:S(2)}, u32[]{:S(2)}) %collective-permute-start.13) | collective-permute-done | bytes 122912 | tf_op jit(solution)/shard_map/ppermute | solution.py:30
  119.4 0.5 fusion.21
  120.3 1.5 %collective-permute-start.18 = (bf16[64,1024]{1,0:T(8,128)(2,1)S(1)}, bf16[64,1024]{1,0:T(8,128)(2,1)S(1)}, u32[]{:S(2)}, u32[]{:S(2)}) collective-permute-start(bf16[64,1024]{1,0:T(8,128)(2,1)S(1)} %fusion.33), channel_id=1, source_target_pairs={{0,2},{1,3},{2,0},{3,1},{4,6},{5,7},{6,4},{7,5},{8,10},{9,11},{10,... | collective-permute-start | bytes 393224 | tf_op jit(solution)/shard_map/ppermute | solution.py:30
  121.8 0.1 fusion.32
  121.9 4.4 %collective-permute-done.18 = bf16[64,1024]{1,0:T(8,128)(2,1)S(1)} collective-permute-done((bf16[64,1024]{1,0:T(8,128)(2,1)S(1)}, bf16[64,1024]{1,0:T(8,128)(2,1)S(1)}, u32[]{:S(2)}, u32[]{:S(2)}) %collective-permute-start.18) | collective-permute-done | bytes 131104 | tf_op jit(solution)/shard_map/ppermute | solution.py:30
  126.3 1.5 %collective-permute-start.20 = (bf16[64,1024]{1,0:T(8,128)(2,1)S(1)}, bf16[64,1024]{1,0:T(8,128)(2,1)S(1)}, u32[]{:S(2)}, u32[]{:S(2)}) collective-permute-start(bf16[64,1024]{1,0:T(8,128)(2,1)S(1)} %fusion.32), channel_id=1, source_target_pairs={{0,2},{1,3},{2,0},{3,1},{4,6},{5,7},{6,4},{7,5},{8,10},{9,11},{10,... | collective-permute-start | bytes 393224 | tf_op jit(solution)/shard_map/ppermute | solution.py:30
  127.8 1.5 %collective-permute-start.19 = (bf16[64,1024]{1,0:T(8,128)(2,1)S(1)}, bf16[64,1024]{1,0:T(8,128)(2,1)S(1)}, u32[]{:S(2)}, u32[]{:S(2)}) collective-permute-start(bf16[64,1024]{1,0:T(8,128)(2,1)S(1)} %fusion.29.p0), channel_id=1, source_target_pairs={{0,6},{1,7},{2,4},{3,5},{4,2},{5,3},{6,0},{7,1},{8,14},{9,15},{10,... | collective-permute-start | bytes 393224 | tf_op jit(solution)/shard_map/ppermute | solution.py:30
  129.2 2.8 %collective-permute-done.20 = bf16[64,1024]{1,0:T(8,128)(2,1)S(1)} collective-permute-done((bf16[64,1024]{1,0:T(8,128)(2,1)S(1)}, bf16[64,1024]{1,0:T(8,128)(2,1)S(1)}, u32[]{:S(2)}, u32[]{:S(2)}) %collective-permute-start.20) | collective-permute-done | bytes 131104 | tf_op jit(solution)/shard_map/ppermute | solution.py:30
  132.1 0.1 fusion.27
  132.2 0.7 collective-permute-start.21
  132.9 3.8 %collective-permute-start.22 = (bf16[64,1024]{1,0:T(8,128)(2,1)S(1)}, bf16[64,1024]{1,0:T(8,128)(2,1)S(1)}, u32[]{:S(2)}, u32[]{:S(2)}) collective-permute-start(bf16[64,1024]{1,0:T(8,128)(2,1)S(1)} %fusion.27), channel_id=1, source_target_pairs={{0,14},{1,15},{2,12},{3,13},{4,10},{5,11},{6,8},{7,9},{8,6},{9,7},... | collective-permute-start | bytes 393224 | tf_op jit(solution)/shard_map/ppermute | solution.py:30
  136.7 0.6 dynamic_slice.26
  138.0 3.0 %collective-permute-done.22.p3 = bf16[64,1024]{1,0:T(8,128)(2,1)S(1)} collective-permute-done((bf16[64,1024]{1,0:T(8,128)(2,1)S(1)}, bf16[64,1024]{1,0:T(8,128)(2,1)S(1)}, u32[]{:S(2)}, u32[]{:S(2)}) %collective-permute-start.22) | collective-permute-done | bytes 131104 | tf_op jit(solution)/shard_map/ppermute | solution.py:30
  141.1 1.4 shard_map.121
  (63 shorter events, 1.0 us)
Async XLA Ops:
  0.0 47.2 %copy-start = (bf16[1280,320]{0,1:T(8,128)(2,1)S(1)}, bf16[1280,320]{0,1:T(8,128)(2,1)}, u32[]{:S(2)}) copy-start(bf16[1280,320]{0,1:T(8,128)(2,1)} %param.18) | copy-start | bytes 2457604
  2.0 6.5 %copy-start.6 = (f32[3,320]{1,0:T(4,128)S(1)}, f32[3,320]{1,0:T(4,128)}, u32[]{:S(2)}) copy-start(f32[3,320]{1,0:T(4,128)} %param.17) | copy-start | bytes 11524
  2.0 6.6 %copy-start.4 = (f32[1280]{0:T(1024)S(1)}, f32[1280]{0:T(1024)}, u32[]{:S(2)}) copy-start(f32[1280]{0:T(1024)} %param.14) | copy-start | bytes 15364
  2.0 6.6 %copy-start.5 = (f32[1280]{0:T(1024)S(1)}, f32[1280]{0:T(1024)}, u32[]{:S(2)}) copy-start(f32[1280]{0:T(1024)} %param.15) | copy-start | bytes 15364
  2.0 11.1 %collective-permute-start = (bf16[320,512]{1,0:T(8,128)(2,1)}, bf16[320,512]{1,0:T(8,128)(2,1)}, u32[]{:S(2)}, u32[]{:S(2)}) collective-permute-start(bf16[320,512]{1,0:T(8,128)(2,1)} %get-tuple-element.15), channel_id=1, source_target_pairs={{0,4},{1,5},{2,6},{3,7},{4,0},{5,1},{6,2},{7,3},{8,12},{9,13},{10,... | collective-permute-start | bytes 983048 | tf_op jit(solution)/shard_map/ppermute | solution.py:30
  6.5 1.7 %copy-start.1 = (bf16[1280,3,320]{0,2,1:T(8,128)(2,1)S(1)}, bf16[1280,3,320]{0,2,1:T(8,128)(2,1)}, u32[]{:S(2)}) copy-start(bf16[1280,3,320]{0,2,1:T(8,128)(2,1)} %param.16) | copy-start | bytes 7372804
  14.1 18.0 %copy-start.2 = (bf16[320,512]{1,0:T(8,128)(2,1)}, bf16[320,512]{1,0:T(8,128)(2,1)S(1)}, u32[]{:S(2)}) copy-start(bf16[320,512]{1,0:T(8,128)(2,1)S(1)} %broadcast_select_fusion.8.own) | copy-start | bytes 983044
  14.2 8.9 %collective-permute-start.2 = (bf16[320,512]{1,0:T(8,128)(2,1)S(1)}, bf16[320,512]{1,0:T(8,128)(2,1)S(1)}, u32[]{:S(2)}, u32[]{:S(2)}) collective-permute-start(bf16[320,512]{1,0:T(8,128)(2,1)S(1)} %broadcast_select_fusion.8.own), channel_id=1, source_target_pairs={{0,2},{1,3},{2,0},{3,1},{4,6},{5,7},{6,4},{7,5},{8,10},{9,11},{10,... | collective-permute-start | bytes 983048 | tf_op jit(solution)/shard_map/ppermute | solution.py:30
  15.9 28.7 %copy-start.10 = (f32[320]{0:T(512)S(1)}, f32[320]{0:T(512)}, u32[]{:S(2)}) copy-start(f32[320]{0:T(512)} %param.19) | copy-start | bytes 3844
  16.0 7.4 %collective-permute-start.1 = (bf16[320,512]{1,0:T(8,128)(2,1)S(1)}, bf16[320,512]{1,0:T(8,128)(2,1)S(1)}, u32[]{:S(2)}, u32[]{:S(2)}) collective-permute-start(bf16[320,512]{1,0:T(8,128)(2,1)S(1)} %broadcast_select_fusion.8.own), channel_id=1, source_target_pairs={{0,1},{1,0},{2,3},{3,2},{4,5},{5,4},{6,7},{7,6},{8,9},{9,8},{10,11... | collective-permute-start | bytes 983048 | tf_op jit(solution)/shard_map/ppermute | solution.py:30
  23.1 1.6 %collective-permute-start.3 = (bf16[320,512]{1,0:T(8,128)(2,1)S(1)}, bf16[320,512]{1,0:T(8,128)(2,1)S(1)}, u32[]{:S(2)}, u32[]{:S(2)}) collective-permute-start(bf16[320,512]{1,0:T(8,128)(2,1)S(1)} %collective-permute-done.2.far), channel_id=1, source_target_pairs={{0,1},{1,0},{2,3},{3,2},{4,5},{5,4},{6,7},{7,6},{8,9},{9,8},{10,11... | collective-permute-start | bytes 983048 | tf_op jit(solution)/shard_map/ppermute | solution.py:30
  32.1 10.0 %collective-permute-start.4 = (bf16[320,512]{1,0:T(8,128)(2,1)}, bf16[320,512]{1,0:T(8,128)(2,1)S(1)}, u32[]{:S(2)}, u32[]{:S(2)}) collective-permute-start(bf16[320,512]{1,0:T(8,128)(2,1)} %shard_map.119), channel_id=1, source_target_pairs={{0,2},{1,3},{2,0},{3,1},{4,6},{5,7},{6,4},{7,5},{8,10},{9,11},{10,... | collective-permute-start | bytes 983048 | tf_op jit(solution)/shard_map/ppermute | solution.py:30
  33.6 12.5 %collective-permute-start.6 = (bf16[320,512]{1,0:T(8,128)(2,1)}, bf16[320,512]{1,0:T(8,128)(2,1)S(1)}, u32[]{:S(2)}, u32[]{:S(2)}) collective-permute-start(bf16[320,512]{1,0:T(8,128)(2,1)} %shard_map.119), channel_id=1, source_target_pairs={{0,1},{1,0},{2,3},{3,2},{4,5},{5,4},{6,7},{7,6},{8,9},{9,8},{10,11... | collective-permute-start | bytes 983048 | tf_op jit(solution)/shard_map/ppermute | solution.py:30
  42.1 4.0 %collective-permute-start.5 = (bf16[320,512]{1,0:T(8,128)(2,1)S(1)}, bf16[320,512]{1,0:T(8,128)(2,1)S(1)}, u32[]{:S(2)}, u32[]{:S(2)}) collective-permute-start(bf16[320,512]{1,0:T(8,128)(2,1)S(1)} %collective-permute-done.4), channel_id=1, source_target_pairs={{0,1},{1,0},{2,3},{3,2},{4,5},{5,4},{6,7},{7,6},{8,9},{9,8},{10,11... | collective-permute-start | bytes 983048 | tf_op jit(solution)/shard_map/ppermute | solution.py:30
  42.1 60.4 %collective-permute-start.11 = (bf16[4,320,512]{2,1,0:T(8,128)(2,1)}, bf16[4,320,512]{2,1,0:T(8,128)(2,1)S(1)}, u32[]{:S(2)}, u32[]{:S(2)}) collective-permute-start(bf16[4,320,512]{2,1,0:T(8,128)(2,1)} %param.22), channel_id=1, source_target_pairs={{0,16},{1,17},{2,18},{3,19},{4,20},{5,21},{6,22},{7,23},{8,24},{9,... | collective-permute-start | bytes 3932168 | tf_op jit(solution)/shard_map/ppermute | solution.py:30
  47.2 5.5 %copy-start.7 = (f32[320]{0:T(512)S(1)}, f32[320]{0:T(512)}, u32[]{:S(2)}) copy-start(f32[320]{0:T(512)} %param.21) | copy-start | bytes 3844
  47.2 5.5 %copy-start.8 = (f32[320]{0:T(512)S(1)}, f32[320]{0:T(512)}, u32[]{:S(2)}) copy-start(f32[320]{0:T(512)} %param.20) | copy-start | bytes 3844
  47.2 7.3 %copy-start.3 = (f32[4096]{0:T(1024)S(1)}, f32[4096]{0:T(1024)}, u32[]{:S(2)}) copy-start(f32[4096]{0:T(1024)} %param.23) | copy-start | bytes 49156
  47.9 1.9 %collective-permute-start.7 = (f32[2,512]{1,0:T(2,128)S(1)}, f32[2,512]{1,0:T(2,128)S(1)}, u32[]{:S(2)}, u32[]{:S(2)}) collective-permute-start(f32[2,512]{1,0:T(2,128)S(1)} %pad_maximum_fusion), channel_id=1, source_target_pairs={{0,1},{1,0},{2,3},{3,2},{4,5},{5,4},{6,7},{7,6},{8,9},{9,8},{10,11... | collective-permute-start | bytes 12296 | tf_op jit(solution)/shard_map/ppermute | solution.py:30
  48.2 3.6 %collective-permute-start.8 = (f32[2,512]{1,0:T(2,128)S(1)}, f32[2,512]{1,0:T(2,128)S(1)}, u32[]{:S(2)}, u32[]{:S(2)}) collective-permute-start(f32[2,512]{1,0:T(2,128)S(1)} %pad_maximum_fusion), channel_id=1, source_target_pairs={{0,2},{1,3},{2,0},{3,1},{4,6},{5,7},{6,4},{7,5},{8,10},{9,11},{10,... | collective-permute-start | bytes 12296 | tf_op jit(solution)/shard_map/ppermute | solution.py:30
  49.6 3.0 %collective-permute-start.9 = (f32[2,512]{1,0:T(2,128)S(1)}, f32[2,512]{1,0:T(2,128)S(1)}, u32[]{:S(2)}, u32[]{:S(2)}) collective-permute-start(f32[2,512]{1,0:T(2,128)S(1)} %pad_maximum_fusion), channel_id=1, source_target_pairs={{0,3},{1,2},{2,1},{3,0},{4,7},{5,6},{6,5},{7,4},{8,11},{9,10},{10,... | collective-permute-start | bytes 12296 | tf_op jit(solution)/shard_map/ppermute | solution.py:30
  52.9 51.7 %collective-permute-start.14 = (bf16[1280,128]{1,0:T(8,128)(2,1)S(1)}, bf16[1280,128]{1,0:T(8,128)(2,1)S(1)}, u32[]{:S(2)}, u32[]{:S(2)}) collective-permute-start(bf16[1280,128]{1,0:T(8,128)(2,1)S(1)} %bitcast.109), channel_id=1, source_target_pairs={{0,4},{1,5},{2,6},{3,7},{4,0},{5,1},{6,2},{7,3},{8,12},{9,13},{10,... | collective-permute-start | bytes 983048 | tf_op jit(solution)/shard_map/ppermute | solution.py:30
  103.8 10.6 %collective-permute-start.10 = (bf16[1280,128]{1,0:T(8,128)(2,1)S(1)}, bf16[1280,128]{1,0:T(8,128)(2,1)S(1)}, u32[]{:S(2)}, u32[]{:S(2)}) collective-permute-start(bf16[1280,128]{1,0:T(8,128)(2,1)S(1)} %bitcast.110), channel_id=1, source_target_pairs={{0,8},{1,9},{2,10},{3,11},{4,12},{5,13},{6,14},{7,15},{8,0},{9,1},... | collective-permute-start | bytes 983048 | tf_op jit(solution)/shard_map/ppermute | solution.py:30
  105.5 14.6 %collective-permute-start.17 = (bf16[2,64,1024]{2,1,0:T(8,128)(2,1)S(1)}, bf16[2,64,1024]{2,1,0:T(8,128)(2,1)S(1)}, u32[]{:S(2)}, u32[]{:S(2)}) collective-permute-start(bf16[2,64,1024]{2,1,0:T(8,128)(2,1)S(1)} %fusion.25), channel_id=1, source_target_pairs={{0,1},{1,0},{2,3},{3,2},{4,5},{5,4},{6,7},{7,6},{8,9},{9,8},{10,11... | collective-permute-start | bytes 786440 | tf_op jit(solution)/shard_map/ppermute | solution.py:30
  105.6 13.8 %collective-permute-start.15 = (bf16[800,128]{1,0:T(8,128)(2,1)S(1)}, bf16[800,128]{1,0:T(8,128)(2,1)S(1)}, u32[]{:S(2)}, u32[]{:S(2)}) collective-permute-start(bf16[800,128]{1,0:T(8,128)(2,1)S(1)} %slice.78), channel_id=1, source_target_pairs={{0,8},{1,9},{2,10},{3,11},{4,12},{5,13},{6,14},{7,15},{8,0},{9,1},... | collective-permute-start | bytes 614408 | tf_op jit(solution)/shard_map/ppermute | solution.py:30
  114.5 4.9 %collective-permute-start.13 = (bf16[480,128]{1,0:T(8,128)(2,1)S(1)}, bf16[480,128]{1,0:T(8,128)(2,1)S(1)}, u32[]{:S(2)}, u32[]{:S(2)}) collective-permute-start(bf16[480,128]{1,0:T(8,128)(2,1)S(1)} %slice.77), channel_id=1, source_target_pairs={{0,4},{1,5},{2,6},{3,7},{4,0},{5,1},{6,2},{7,3},{8,12},{9,13},{10,... | collective-permute-start | bytes 368648 | tf_op jit(solution)/shard_map/ppermute | solution.py:30
  116.6 5.2 %collective-permute-start.12 = (bf16[1,64,1024]{2,1,0:T(8,128)(2,1)S(1)}, bf16[1,64,1024]{2,1,0:T(8,128)(2,1)S(1)}, u32[]{:S(2)}, u32[]{:S(2)}) collective-permute-start(bf16[1,64,1024]{2,1,0:T(8,128)(2,1)S(1)} %fusion.30), channel_id=1, source_target_pairs={{0,1},{1,0},{2,3},{3,2},{4,5},{5,4},{6,7},{7,6},{8,9},{9,8},{10,11... | collective-permute-start | bytes 393224 | tf_op jit(solution)/shard_map/ppermute | solution.py:30
  120.0 16.7 %copy-start.9 = (s32[16]{0:T(128)S(1)}, s32[16]{0:T(128)}, u32[]{:S(2)}) copy-start(s32[16]{0:T(128)} %param.13) | copy-start | bytes 196
  120.0 1.7 %collective-permute-start.16 = (bf16[1,64,1024]{2,1,0:T(8,128)(2,1)S(1)}, bf16[1,64,1024]{2,1,0:T(8,128)(2,1)S(1)}, u32[]{:S(2)}, u32[]{:S(2)}) collective-permute-start(bf16[1,64,1024]{2,1,0:T(8,128)(2,1)S(1)} %fusion.31), channel_id=1, source_target_pairs={{0,1},{1,0},{2,3},{3,2},{4,5},{5,4},{6,7},{7,6},{8,9},{9,8},{10,11... | collective-permute-start | bytes 393224 | tf_op jit(solution)/shard_map/ppermute | solution.py:30
  120.3 6.0 %collective-permute-start.18 = (bf16[64,1024]{1,0:T(8,128)(2,1)S(1)}, bf16[64,1024]{1,0:T(8,128)(2,1)S(1)}, u32[]{:S(2)}, u32[]{:S(2)}) collective-permute-start(bf16[64,1024]{1,0:T(8,128)(2,1)S(1)} %fusion.33), channel_id=1, source_target_pairs={{0,2},{1,3},{2,0},{3,1},{4,6},{5,7},{6,4},{7,5},{8,10},{9,11},{10,... | collective-permute-start | bytes 393224 | tf_op jit(solution)/shard_map/ppermute | solution.py:30
  126.3 5.8 %collective-permute-start.20 = (bf16[64,1024]{1,0:T(8,128)(2,1)S(1)}, bf16[64,1024]{1,0:T(8,128)(2,1)S(1)}, u32[]{:S(2)}, u32[]{:S(2)}) collective-permute-start(bf16[64,1024]{1,0:T(8,128)(2,1)S(1)} %fusion.32), channel_id=1, source_target_pairs={{0,2},{1,3},{2,0},{3,1},{4,6},{5,7},{6,4},{7,5},{8,10},{9,11},{10,... | collective-permute-start | bytes 393224 | tf_op jit(solution)/shard_map/ppermute | solution.py:30
  127.8 10.3 %collective-permute-start.19 = (bf16[64,1024]{1,0:T(8,128)(2,1)S(1)}, bf16[64,1024]{1,0:T(8,128)(2,1)S(1)}, u32[]{:S(2)}, u32[]{:S(2)}) collective-permute-start(bf16[64,1024]{1,0:T(8,128)(2,1)S(1)} %fusion.29.p0), channel_id=1, source_target_pairs={{0,6},{1,7},{2,4},{3,5},{4,2},{5,3},{6,0},{7,1},{8,14},{9,15},{10,... | collective-permute-start | bytes 393224 | tf_op jit(solution)/shard_map/ppermute | solution.py:30
  132.2 5.9 %collective-permute-start.21 = (bf16[64,1024]{1,0:T(8,128)(2,1)S(1)}, bf16[64,1024]{1,0:T(8,128)(2,1)S(1)}, u32[]{:S(2)}, u32[]{:S(2)}) collective-permute-start(bf16[64,1024]{1,0:T(8,128)(2,1)S(1)} %fusion.27), channel_id=1, source_target_pairs={{0,8},{1,9},{2,10},{3,11},{4,12},{5,13},{6,14},{7,15},{8,0},{9,1},... | collective-permute-start | bytes 393224 | tf_op jit(solution)/shard_map/ppermute | solution.py:30
  132.9 8.2 %collective-permute-start.22 = (bf16[64,1024]{1,0:T(8,128)(2,1)S(1)}, bf16[64,1024]{1,0:T(8,128)(2,1)S(1)}, u32[]{:S(2)}, u32[]{:S(2)}) collective-permute-start(bf16[64,1024]{1,0:T(8,128)(2,1)S(1)} %fusion.27), channel_id=1, source_target_pairs={{0,14},{1,15},{2,12},{3,13},{4,10},{5,11},{6,8},{7,9},{8,6},{9,7},... | collective-permute-start | bytes 393224 | tf_op jit(solution)/shard_map/ppermute | solution.py:30
